TPU v7x, 32 devices: a whole 2x2x4 slice. The times are simulated.
32 devices in a mesh: dp: 8 (over y, x, core), mp: 4 (over z).
Axes of the slice: x: 2, y: 2, z: 4, core: 2. Of those that a mesh axis runs over, the one named last changes fastest.
Arguments:
- acts: bfloat16 [4096, 3072], P('dp'), may hold values from -16 to 16
- grads_out: bfloat16 [4096, 8192], P('dp', 'mp'), may hold values from -0.125 to 0.125
- old_a: float32 [8, 3, 128, 1024], P('dp'), may hold values from -0.09375 to 0.09375
- old_g: float32 [4, 8, 2, 128, 1024], P('mp', 'dp'), may hold values from -0.09375 to 0.09375
- a_inverse: bfloat16 [3072, 1024], P('dp'), may hold values from -0.1875 to 0.1875
- g_inverse: bfloat16 [8192, 1024], P('mp'), may hold values from -0.1875 to 0.1875
- owner_map: int32 [5, 8], replicated, may hold values from 0 to 7, each once within a row
Outputs:
- a_factor: float32 [8, 3, 128, 1024], P('dp')
- g_factor: float32 [4, 8, 2, 128, 1024], P('mp', 'dp')
- preconditioned: bfloat16 [3072, 4, 2048], P(None, 'mp', 'dp')
Inputs may be any that keep to these rules, and one draw needn't show every extreme that they name: `owner_map`: each row is a permutation: row k tells, for each of the 8 row strips of factor block k, which dp index holds it. Rows 0 to 2 are the activation blocks, the others the output-gradient blocks of every mp index.
All inputs are finite; a program needn't handle non-finite values.
Results may differ from a plain program's by a relative error of at most 0.02.
Values may be sent and summed in bfloat16 or wider, within the bound.
A program may use at most 128 MiB of HBM per device.

v0:
```python
import functools

import jax
import jax.numpy as jnp
from jax import lax
from jax.experimental import pallas as pl
from jax.experimental.pallas import tpu as pltpu
from jax.sharding import PartitionSpec as P

decay_rate = 0.75
low = jnp.bfloat16
full = jnp.float32


def chip_at(me, slot, order):
    chip = 0
    for place, bit in enumerate(order):
        want = lax.rem(lax.div(jnp.int32(slot), jnp.int32(1 << (len(order) - 1 - place))), jnp.int32(2))
        have = lax.rem(lax.div(me, jnp.int32(1 << bit)), jnp.int32(2))
        chip = chip + (want + have - 2 * want * have) * (1 << bit)
    return chip


def slot_of(relative, order):
    slot = 0
    for place, bit in enumerate(order):
        slot += ((relative >> bit) & 1) << (len(order) - 1 - place)
    return slot


def kernel(
    sizes, owner_map, acts, grads, a_inverse, g_inverse, out, g_cov, a_cov,
    acts2, grads2, g_cols, turned, a_all, flipped, wide, right, out_tile, g_sum, a_rows,
    grad_part, g_part, a_part, grad_came, g_came, a_came, local_sem, send_sem, recv_sem,
):
    dp_count, mp_count, tokens = sizes
    chips = dp_count // 2
    bits = list(range(chips.bit_length() - 1))
    orders = (bits, bits[::-1])
    stages = len(bits)
    own, features = acts.shape
    hidden = grads.shape[1]
    block = a_inverse.shape[1]
    na, ng = features // block, hidden // block
    strip = block // dp_count
    sub = strip // mp_count
    width = hidden // dp_count
    half = block // 2
    shard = a_inverse.shape[0]
    piece = block // mp_count

    dp = lax.axis_index("dp")
    mp = lax.axis_index("mp")
    chip, core = lax.div(dp, jnp.int32(2)), lax.rem(dp, jnp.int32(2))
    partner = (chip * 2 + 1 - core, mp)
    relatives = [chip_at(chip, r, bits[::-1]) for r in range(chips)]
    above = [lax.rem(mp + step, jnp.int32(mp_count)) for step in range(mp_count)]

    sent = []

    def send(src, dst, device):
        place = len(sent)
        copy = pltpu.make_async_remote_copy(
            src_ref=src, dst_ref=dst, send_sem=send_sem.at[place], recv_sem=recv_sem.at[place],
            device_id=device, device_id_type=pl.DeviceIdType.MESH,
        )
        copy.start()
        sent.append(copy)
        return copy

    placed = []

    def move(src, dst):
        copy = pltpu.make_async_copy(src, dst, local_sem.at[len(placed)])
        copy.start()
        placed.append(copy)
        return copy

    def rows_of(chip_index, core_index):
        return pl.ds(pl.multiple_of((chip_index * 2 + core_index) * shard, shard), shard)

    my_piece = pl.ds(pl.multiple_of(mp * piece, piece), piece)

    load_acts = move(acts, acts2.at[:own])
    load_grads = move(grads, grads2.at[:own])
    load_cols = [
        move(
            g_inverse.at[:, pl.ds(pl.multiple_of((2 * u + core) * width, width), width)],
            g_cols.at[:, u * width : (u + 1) * width],
        )
        for u in range(block // width // 2)
    ]
    load_inverse = move(a_inverse, a_all.at[rows_of(chip, core)])

    barrier = pltpu.get_barrier_semaphore()
    peers = [partner]
    peers += [(q * 2 + core, mp) for q in relatives[1:]]
    peers += [(dp, m) for m in above[1:]]
    for peer in peers:
        pl.semaphore_signal(barrier, inc=1, device_id=peer, device_id_type=pl.DeviceIdType.MESH)
    pl.semaphore_wait(barrier, len(peers))

    other_acts = send(acts, acts2.at[own:], partner)
    other_grads = send(grads, grads2.at[own:], partner)
    spread = [
        send(a_inverse.at[:, my_piece], a_all.at[rows_of(chip, core), my_piece], (q * 2 + core, mp))
        for q in relatives[1:]
    ]
    crossed = [send(a_inverse, a_all.at[rows_of(chip, core)], partner)]

    def start(part, came, stage):
        first, last = chips >> (stage + 1), chips >> stage
        copies = []
        for side in range(2):
            bit = orders[side][stage]
            peer = (chip_at(chip, 1 << bit, bits[::-1]) * 2 + core, mp)
            copies.append(send(part.at[side, first:last], came[stage].at[side], peer))
        return copies

    def add(part, came, stage, copies):
        for side in range(2):
            copies[side].wait_recv()
            count = chips >> (stage + 1)

            def one(slot, unused):
                total = part[side, slot].astype(full) + came[stage][side, slot].astype(full)
                part[side, slot] = total.astype(low)
                return unused

            lax.fori_loop(0, count, one, 0)

    def advance(part, came, copies):
        for stage in range(stages - 1):
            add(part, came, stage, copies)
            copies = start(part, came, stage + 1)
        return copies

    def flip_strips(source, block_index, row):
        for r in range(chips):
            owner = relatives[r] * 2 + core
            span = max(strip, 128)
            rows = None
            for start_at in range(0, block, span):
                cols = source[:, pl.ds(pl.multiple_of(block_index * block + start_at, span), span)]
                held = owner_map[row, start_at // strip]
                for inner in range(1, span // strip):
                    held = jnp.where(owner_map[row, start_at // strip + inner] == owner, owner, held)
                rows = cols if rows is None else lax.select(held == owner, cols, rows)
            rows = rows.T
            for inner in range(span // strip):
                part = rows[inner * strip : (inner + 1) * strip]
                if inner == 0:
                    chosen = part
                    continue
                here = jnp.int32(0)
                for s in range(inner, dp_count, span // strip):
                    here = here + jnp.where(owner_map[row, s] == owner, jnp.int32(1), jnp.int32(0))
                chosen = lax.select(here == 1, part, chosen)
            flipped[r * strip : (r + 1) * strip, :] = chosen

    load_acts.wait()
    other_acts.wait_recv()

    def a_block(k, unused):
        flip_strips(acts2, k, k)
        for side in range(2):
            cols = pl.ds(pl.multiple_of(k * block + side * half, half), half)
            wide[...] = jnp.dot(flipped[...], acts2[:, cols], preferred_element_type=full)
            for r in range(chips):
                rows = wide[pl.ds(pl.multiple_of(r * strip + mp * sub, sub), sub), :]
                a_part[side, slot_of(r, orders[side]), k] = (rows / tokens).astype(low)
        return unused

    lax.fori_loop(0, na, a_block, 0)
    a_copies = start(a_part, a_came, 0)

    load_grads.wait()
    other_grads.wait_recv()
    for copy in load_cols:
        copy.wait()

    def turn(j, unused):
        rows = pl.ds(pl.multiple_of(j * block, block), block)
        cols = pl.ds(pl.multiple_of(j * half, half), half)
        turned[:, cols] = jnp.dot(
            grads2[:, rows], g_cols[rows, :], preferred_element_type=full
        ).astype(low)
        return unused

    lax.fori_loop(0, ng, turn, 0)

    def multiply(k):
        for side in range(2):

            def flip_one(v, unused):
                cols = pl.ds(pl.multiple_of(k * block + side * half + v * 128, 128), 128)
                flipped[pl.ds(pl.multiple_of(v * 128, 128), 128), :] = acts2[:, cols].T
                return unused

            lax.fori_loop(0, half // 128, flip_one, 0)

            def product(slot, unused):
                q = chip_at(chip, slot, orders[side])
                cols = pl.ds(pl.multiple_of(q * width, width), width)
                grad_part[k, side, slot] = jnp.dot(
                    flipped[...], turned[:, cols], preferred_element_type=full
                ).astype(low)
                return unused

            lax.fori_loop(0, chips, product, 0)
        return start(grad_part.at[k], [came.at[k] for came in grad_came], 0)

    def advance_grad(k, copies):
        return advance(grad_part.at[k], [came.at[k] for came in grad_came], copies)

    grad_copies = [None] * na
    grad_copies[0] = multiply(0)

    climbed = []
    load_inverse.wait()
    for r in range(1, chips):
        spread[r - 1].wait_recv()
        for m in above[1:]:
            where = a_all.at[rows_of(relatives[r], core), my_piece]
            climbed.append(send(where, where, (dp, m)))

    a_copies = advance(a_part, a_came, a_copies)
    gathered = None
    for k in range(1, na):
        grad_copies[k] = multiply(k)
        grad_copies[k - 1] = advance_grad(k - 1, grad_copies[k - 1])
        if k == 1:
            for side in range(2):
                a_copies[side].wait_recv()
            for side in range(2):
                total = a_part[side, 0].astype(full) + a_came[-1][side, 0].astype(full)
                a_rows[mp, :, :, side * half : (side + 1) * half] = total.astype(low)
            gathered = [send(a_rows.at[mp], a_rows.at[mp], (dp, m)) for m in above[1:]]

    def g_block(j, unused):
        flip_strips(grads2, j, na + j)
        for side in range(2):
            cols = pl.ds(pl.multiple_of(j * block + side * half, half), half)
            wide[...] = jnp.dot(flipped[...], grads2[:, cols], preferred_element_type=full)
            for r in range(chips):
                rows = wide[r * strip : (r + 1) * strip, :]
                g_part[side, slot_of(r, orders[side]), j] = rows.astype(low)
        return unused

    lax.fori_loop(0, ng, g_block, 0)
    g_copies = start(g_part, g_came, 0)
    grad_copies[na - 1] = advance_grad(na - 1, grad_copies[na - 1])

    for r in range(1, chips):
        for step in range(mp_count - 1):
            climbed[(r - 1) * (mp_count - 1) + step].wait_recv()
        where = a_all.at[rows_of(relatives[r], core)]
        crossed.append(send(where, where, partner))

    g_copies = advance(g_part, g_came, g_copies)

    for copy in crossed:
        copy.wait_recv()
    for k in range(na):
        for side in range(2):
            grad_copies[k][side].wait_recv()
            total = grad_part[k, side, 0].astype(full) + grad_came[-1][k, side, 0].astype(full)
            right[side * half : (side + 1) * half, :] = total.astype(low)

        def finish(t, unused):
            rows = pl.ds(pl.multiple_of(k * block + t * 256, 256), 256)
            out_tile[rows, :] = jnp.dot(
                a_all[rows, :], right[...], preferred_element_type=full
            ).astype(low)
            return unused

        lax.fori_loop(0, block // 256, finish, 0)
        done = slice(k * block, (k + 1) * block)
        move(out_tile.at[done], out.at[done])

    for copy in gathered:
        copy.wait_recv()
    move(a_rows, a_cov)
    for side in range(2):
        g_copies[side].wait_recv()
        total = g_part[side, 0].astype(full) + g_came[-1][side, 0].astype(full)
        g_sum[:, :, side * half : (side + 1) * half] = total.astype(low)
    move(g_sum, g_cov)
    for copy in placed[-(na + 2) :]:
        copy.wait()
    for copy in sent:
        copy.wait_send()


def per_device(acts, grads_out, old_a, old_g, a_inverse, g_inverse, owner_map):
    dp_count = lax.axis_size("dp")
    mp_count = lax.axis_size("mp")
    chips = dp_count // 2
    stages = chips.bit_length() - 1
    own, features = acts.shape
    hidden = grads_out.shape[1]
    block = a_inverse.shape[1]
    na, ng = features // block, hidden // block
    strip = block // dp_count
    sub = strip // mp_count
    width = hidden // dp_count
    half = block // 2
    copies = 2 + (chips - 1) * (mp_count + 1) + 1 + (na + 2) * 2 * stages + mp_count - 1
    loads = 3 + block // width // 2 + na + 2

    def came(*shape):
        return [pltpu.VMEM((*shape[0], chips >> (s + 1), *shape[1]), low) for s in range(stages)]

    scratch = [
        pltpu.VMEM((2 * own, features), low),
        pltpu.VMEM((2 * own, hidden), low),
        pltpu.VMEM((hidden, half), low),
        pltpu.VMEM((2 * own, hidden // 2), low),
        pltpu.VMEM((features, block), low),
        pltpu.VMEM((half, 2 * own), low),
        pltpu.VMEM((half, half), full),
        pltpu.VMEM((block, width), low),
        pltpu.VMEM((features, width), low),
        pltpu.VMEM((ng, strip, block), low),
        pltpu.VMEM((mp_count, na, sub, block), low),
        pltpu.VMEM((na, 2, chips, half, width), low),
        pltpu.VMEM((2, chips, ng, strip, half), low),
        pltpu.VMEM((2, chips, na, sub, half), low),
        came((na, 2), (half, width)),
        came((2,), (ng, strip, half)),
        came((2,), (na, sub, half)),
        pltpu.SemaphoreType.DMA((loads,)),
        pltpu.SemaphoreType.DMA((copies,)),
        pltpu.SemaphoreType.DMA((copies,)),
    ]
    anywhere = pl.BlockSpec(memory_space=pl.ANY)
    out, g_cov, a_cov = pl.pallas_call(
        functools.partial(kernel, (dp_count, mp_count, own * dp_count)),
        out_shape=(
            jax.ShapeDtypeStruct((features, width), low),
            jax.ShapeDtypeStruct((ng, strip, block), low),
            jax.ShapeDtypeStruct((mp_count, na, sub, block), low),
        ),
        in_specs=[pl.BlockSpec(memory_space=pltpu.SMEM)] + [anywhere] * 4,
        out_specs=(anywhere,) * 3,
        scratch_shapes=scratch,
        compiler_params=pltpu.CompilerParams(
            collective_id=0, has_side_effects=True, vmem_limit_bytes=60 * 1024 * 1024
        ),
        name="step",
    )(owner_map, acts, grads_out, a_inverse, g_inverse)
    a_cov = a_cov.transpose(1, 0, 2, 3).reshape(old_a.shape).astype(full)
    g_cov = g_cov.reshape(old_g.shape).astype(full)
    a_factor = decay_rate * old_a + (1.0 - decay_rate) * a_cov
    g_factor = decay_rate * old_g + (1.0 - decay_rate) * g_cov
    return (a_factor, g_factor, out.reshape(features, 1, width))


def solution(mesh):
    placed = (
        P("dp", None),
        P("dp", "mp"),
        P("dp", None, None, None),
        P("mp", "dp", None, None, None),
        P("dp", None),
        P("mp", None),
        P(),
    )
    return jax.shard_map(
        per_device,
        mesh=mesh,
        in_specs=placed,
        out_specs=(P("dp", None, None, None), P("mp", "dp", None, None, None), P(None, "mp", "dp")),
        check_vma=False,
    )
```

profile of v0, /device:TPU:0, one launch (start us, length us, event | category | flops | bytes accessed | tf_op | source)
XLA Modules:
  0.0 109.2 jit_solution(2250677194259085247)
XLA Ops:
  0.6 101.8 %step.1 = (bf16[3072,256]{1,0:T(8,128)(2,1)}, bf16[2,128,1024]{2,1,0:T(8,128)(2,1)}, bf16[4,3,32,1024]{3,2,1,0:T(8,128)(2,1)}) custom-call(s32[5,8]{1,0:T(8,128)} %owner_map.1, bf16[512,3072]{1,0:T(8,128)(2,1)} %acts.1, bf16[512,2048]{1,0:T(8,128)(2,1)} %grads.1, bf16[384,1024]{1,0:T(8,128)(2,1)} %a_inverse.1, bf16[2048,1024]{1,0:T(8,128)(2,1)} %g_inverse.1), custom_call_target="tpu_custom_call" | custom-call | tf_op jit(solution)/shard_map/step/pallas_call | solution.py:337
  102.4 1.3 %multiply_bitcast_fusion = f32[3,4,32,1024]{3,2,0,1:T(8,128)S(1)} fusion(bf16[4,3,32,1024]{3,2,1,0:T(8,128)(2,1)} %get-tuple-element.6), kind=kLoop, calls=%fused_computation | loop fusion | flops 786432 | bytes 2359296 | tf_op jit(solution)/shard_map/mul | solution.py:354
  103.8 0.0 copy-start.1
  103.8 0.2 copy.10
  103.9 1.2 %copy-done.1 = f32[1,3,128,1024]{3,2,1,0:T(8,128)S(1)} copy-done((f32[1,3,128,1024]{3,2,1,0:T(8,128)S(1)}, f32[1,3,128,1024]{3,2,1,0:T(8,128)}, u32[]{:S(2)}) %copy-start.1) | copy-done | bytes 1572888
  105.2 0.0 copy-start.2
  105.2 0.0 copy-start.3
  105.2 1.4 %multiply_add_fusion = f32[1,3,128,1024]{3,2,1,0:T(8,128)} fusion(f32[1,3,128,1024]{3,2,1,0:T(8,128)S(1)} %bitcast.6, f32[1,3,128,1024]{3,2,1,0:T(8,128)S(1)} %copy-done.1), kind=kLoop, calls=%fused_computation.1 | loop fusion | flops 786432 | bytes 4718592 | tf_op jit(solution)/shard_map/add | solution.py:354
  106.6 0.0 copy-start
  106.6 0.0 copy-done.2
  106.6 0.3 copy-done.3
  106.9 1.1 %bitcast_add_fusion = f32[1,1,2,128,1024]{4,3,2,1,0:T(8,128)} fusion(bf16[2,128,1024]{2,1,0:T(8,128)(2,1)S(1)} %copy-done.3, f32[1,1,2,128,1024]{4,3,2,1,0:T(8,128)S(1)} %copy-done.2), kind=kLoop, calls=%fused_computation.2 | loop fusion | flops 1048576 | bytes 2621440 | tf_op jit(solution)/shard_map/add | solution.py:355
  108.1 0.0 copy-done
  108.1 1.1 %copy.12 = bf16[3072,1,256]{2,0,1:T(8,128)(2,1)} copy(bf16[3072,1,256]{2,0,1:T(8,128)(2,1)S(1)} %bitcast.7) | data formatting | bytes 3145728
Async XLA Ops:
  103.8 1.4 %copy-start.1 = (f32[1,3,128,1024]{3,2,1,0:T(8,128)S(1)}, f32[1,3,128,1024]{3,2,1,0:T(8,128)}, u32[]{:S(2)}) copy-start(f32[1,3,128,1024]{3,2,1,0:T(8,128)} %param.9) | copy-start | bytes 4718596
  105.2 1.4 %copy-start.2 = (f32[1,1,2,128,1024]{4,3,2,1,0:T(8,128)S(1)}, f32[1,1,2,128,1024]{4,3,2,1,0:T(8,128)}, u32[]{:S(2)}) copy-start(f32[1,1,2,128,1024]{4,3,2,1,0:T(8,128)} %param.10) | copy-start | bytes 3145732
  105.2 1.8 %copy-start.3 = (bf16[2,128,1024]{2,1,0:T(8,128)(2,1)S(1)}, bf16[2,128,1024]{2,1,0:T(8,128)(2,1)}, u32[]{:S(2)}) copy-start(bf16[2,128,1024]{2,1,0:T(8,128)(2,1)} %get-tuple-element.7) | copy-start | bytes 1572868
  106.6 1.5 %copy-start = (bf16[3072,256]{1,0:T(8,128)(2,1)S(1)}, bf16[3072,256]{1,0:T(8,128)(2,1)}, u32[]{:S(2)}) copy-start(bf16[3072,256]{1,0:T(8,128)(2,1)} %get-tuple-element.8) | copy-start | bytes 4718596
where the time goes:
time: 109 us
  Pallas kernels  102 us (94%)
  other arithmetic  3.87 us (4%)
  local copies, waits for them, and re-layouts  2.87 us (3%)
    pallas_call x1, Pallas kernels, per_device(): pl.pallas_call(functools.partial(kernel, (dp_count, mp_count, own * dp_co...  102 us
    unnamed x9, local copies, waits for them, and re-layouts  2.7 us

commit v1 on v0

v1 whole, which is shorter than its diff:
```python
import functools

import jax
import jax.numpy as jnp
from jax import lax
from jax.experimental import pallas as pl
from jax.experimental.pallas import tpu as pltpu
from jax.sharding import PartitionSpec as P

decay_rate = 0.75
low = jnp.bfloat16
full = jnp.float32


def chip_at(me, slot, order):
    chip = 0
    for place, bit in enumerate(order):
        want = lax.rem(lax.div(jnp.int32(slot), jnp.int32(1 << (len(order) - 1 - place))), jnp.int32(2))
        have = lax.rem(lax.div(me, jnp.int32(1 << bit)), jnp.int32(2))
        chip = chip + (want + have - 2 * want * have) * (1 << bit)
    return chip


def slot_of(relative, order):
    slot = 0
    for place, bit in enumerate(order):
        slot += ((relative >> bit) & 1) << (len(order) - 1 - place)
    return slot


def kernel(
    sizes, owner_map, acts, grads, a_inverse, g_inverse, old_a, old_g, out_tile, a_new, g_new,
    acts2, grads2, g_cols, turned, a_all, flipped, wide, right, a_rows, a_old, g_old,
    grad_part, g_part, a_part, grad_came, g_came, a_came, local_sem, send_sem, recv_sem,
):
    dp_count, mp_count, tokens = sizes
    chips = dp_count // 2
    bits = list(range(chips.bit_length() - 1))
    orders = (bits, bits[::-1])
    stages = len(bits)
    own, features = acts.shape
    hidden = grads.shape[1]
    block = a_inverse.shape[1]
    na, ng = features // block, hidden // block
    strip = block // dp_count
    sub = strip // mp_count
    width = hidden // dp_count
    half = block // 2
    shard = a_inverse.shape[0]
    piece = block // mp_count

    dp = lax.axis_index("dp")
    mp = lax.axis_index("mp")
    chip, core = lax.div(dp, jnp.int32(2)), lax.rem(dp, jnp.int32(2))
    partner = (chip * 2 + 1 - core, mp)
    relatives = [chip_at(chip, r, bits[::-1]) for r in range(chips)]
    above = [lax.rem(mp + step, jnp.int32(mp_count)) for step in range(mp_count)]

    sent = []

    def send(src, dst, device):
        place = len(sent)
        copy = pltpu.make_async_remote_copy(
            src_ref=src, dst_ref=dst, send_sem=send_sem.at[place], recv_sem=recv_sem.at[place],
            device_id=device, device_id_type=pl.DeviceIdType.MESH,
        )
        copy.start()
        sent.append(copy)
        return copy

    placed = []

    def move(src, dst):
        copy = pltpu.make_async_copy(src, dst, local_sem.at[len(placed)])
        copy.start()
        placed.append(copy)
        return copy

    def rows_of(chip_index, core_index, part=None):
        first = (chip_index * 2 + core_index) * shard
        if part is None:
            return pl.ds(pl.multiple_of(first, shard), shard)
        return pl.ds(pl.multiple_of(first + part * (shard // 2), shard // 2), shard // 2)

    my_piece = pl.ds(pl.multiple_of(mp * piece, piece), piece)

    load_inverse = move(a_inverse, a_all.at[rows_of(chip, core)])
    load_grads = move(grads, grads2.at[:own])
    load_cols = [
        move(
            g_inverse.at[:, pl.ds(pl.multiple_of((2 * u + core) * width, width), width)],
            g_cols.at[:, u * width : (u + 1) * width],
        )
        for u in range(block // width // 2)
    ]
    load_acts = move(acts, acts2.at[:own])
    load_old_a = move(old_a.at[0], a_old)
    load_old_g = move(old_g.at[0, 0], g_old)

    with jax.named_scope("barrier"):
        barrier = pltpu.get_barrier_semaphore()
        peers = [partner]
        peers += [(q * 2 + core, mp) for q in relatives[1:]]
        peers += [(dp, m) for m in above[1:]]
        for peer in peers:
            pl.semaphore_signal(barrier, inc=1, device_id=peer, device_id_type=pl.DeviceIdType.MESH)
        pl.semaphore_wait(barrier, len(peers))

    other_grads = send(grads, grads2.at[own:], partner)
    other_acts = [
        send(acts.at[:, i * half : (i + 1) * half], acts2.at[own:, i * half : (i + 1) * half], partner)
        for i in range(2 * na)
    ]

    spread = {}
    waited = set()

    def pass_on(stage, relative):
        for side in range(2):
            order = orders[side]
            held = sum(((relative >> i) & 1) << order[i] for i in range(stage))
            peer = (relatives[1 << order[stage]] * 2 + core, mp)
            where = (rows_of(relatives[held], core, side), my_piece)
            if held:
                spread[side, held].wait_recv()
                waited.add((side, held))
            spread[side, held | (1 << order[stage])] = send(a_all.at[where], a_all.at[where], peer)

    load_inverse.wait()
    for stage in range(stages):
        pass_on(stage, 0)
    crossed = [send(a_inverse, a_all.at[rows_of(chip, core)], partner)]

    def start_side(part, came, stage, side):
        first, last = chips >> (stage + 1), chips >> stage
        peer = (relatives[1 << orders[side][stage]] * 2 + core, mp)
        return send(part.at[side, first:last], came[stage].at[side], peer)

    def start(part, came, stage):
        return [start_side(part, came, stage, side) for side in range(2)]

    def add(part, came, stage, copies):
        for side in range(2):
            copies[side].wait_recv()
            count = chips >> (stage + 1)

            def one(slot, unused):
                total = part[side, slot].astype(full) + came[stage][side, slot].astype(full)
                part[side, slot] = total.astype(low)
                return unused

            lax.fori_loop(0, count, one, 0)

    def advance(part, came, copies):
        for stage in range(stages - 1):
            add(part, came, stage, copies)
            copies = start(part, came, stage + 1)
        return copies

    def flip_strips(source, block_index, row):
        for r in range(chips):
            owner = relatives[r] * 2 + core
            span = max(strip, 128)
            rows = None
            for start_at in range(0, block, span):
                cols = source[:, pl.ds(pl.multiple_of(block_index * block + start_at, span), span)]
                held = owner_map[row, start_at // strip]
                for inner in range(1, span // strip):
                    held = jnp.where(owner_map[row, start_at // strip + inner] == owner, owner, held)
                rows = cols if rows is None else lax.select(held == owner, cols, rows)
            rows = rows.T
            for inner in range(span // strip):
                part = rows[inner * strip : (inner + 1) * strip]
                if inner == 0:
                    chosen = part
                    continue
                here = jnp.int32(0)
                for s in range(inner, dp_count, span // strip):
                    here = here + jnp.where(owner_map[row, s] == owner, jnp.int32(1), jnp.int32(0))
                chosen = lax.select(here == 1, part, chosen)
            flipped[0, r * strip : (r + 1) * strip, :] = chosen

    def turn(first):
        def one(j, unused):
            rows = pl.ds(pl.multiple_of(j * block, block), block)
            cols = pl.ds(pl.multiple_of(j * half, half), half)
            turned[first : first + own, cols] = jnp.dot(
                grads2[first : first + own, rows], g_cols[rows, :], preferred_element_type=full
            ).astype(low)
            return unused

        lax.fori_loop(0, ng, one, 0)

    with jax.named_scope("turn_own"):
        load_grads.wait()
        for copy in load_cols:
            copy.wait()
        turn(0)
    with jax.named_scope("pass_on"):
        for stage in range(1, stages):
            for relative in range(1, 1 << stage):
                pass_on(stage, relative)
    with jax.named_scope("turn_other"):
        other_grads.wait_recv()
        turn(own)

    def multiply(k):
        part = grad_part.at[k]
        came = [came.at[k] for came in grad_came]
        copies = []
        for first, last in ((chips // 2, chips), (0, chips // 2)):
            for side in range(2):
                if first:
                    if k < 2:
                        other_acts[2 * k + side].wait_recv()

                    def flip_one(v, unused):
                        cols = pl.ds(pl.multiple_of(k * block + side * half + v * 128, 128), 128)
                        rows = pl.ds(pl.multiple_of(v * 128, 128), 128)
                        flipped[side, rows, :] = acts2[:, cols].T
                        return unused

                    lax.fori_loop(0, half // 128, flip_one, 0)

                def product(slot, unused):
                    q = chip_at(chip, slot, orders[side])
                    cols = pl.ds(pl.multiple_of(q * width, width), width)
                    part[side, slot] = jnp.dot(
                        flipped[side], turned[:, cols], preferred_element_type=full
                    ).astype(low)
                    return unused

                lax.fori_loop(first, last, product, 0)
                if first:
                    copies.append(start_side(part, came, 0, side))
        return copies

    def advance_grad(k, copies):
        return advance(grad_part.at[k], [came.at[k] for came in grad_came], copies)

    def a_block(k, unused):
        flip_strips(acts2, k, k)
        for side in range(2):
            cols = pl.ds(pl.multiple_of(k * block + side * half, half), half)
            wide[...] = jnp.dot(flipped[0], acts2[:, cols], preferred_element_type=full)
            for r in range(chips):
                rows = wide[pl.ds(pl.multiple_of(r * strip + mp * sub, sub), sub), :]
                a_part[side, slot_of(r, orders[side]), k] = (rows / tokens).astype(low)
        return unused

    with jax.named_scope("wait_acts"):
        load_acts.wait()
    grad_copies = [None] * na
    with jax.named_scope("multiply0"):
        grad_copies[0] = multiply(0)

    with jax.named_scope("climb"):
        climbed = []
        for r in range(1, chips):
            for side in range(2):
                if (side, r) not in waited:
                    spread[side, r].wait_recv()
            where = a_all.at[rows_of(relatives[r], core), my_piece]
            climbed.append([send(where, where, (dp, m)) for m in above[1:]])

    for k in range(1, na):
        with jax.named_scope(f"multiply{k}"):
            grad_copies[k] = multiply(k)
        if k == 1:
            with jax.named_scope("a_block"):
                for later in range(4, 2 * na):
                    other_acts[later].wait_recv()
                lax.fori_loop(0, na, a_block, 0)
                a_copies = start(a_part, a_came, 0)
        if k == na - 1:
            with jax.named_scope("advance_a"):
                a_copies = advance(a_part, a_came, a_copies)
        with jax.named_scope(f"advance{k - 1}"):
            grad_copies[k - 1] = advance_grad(k - 1, grad_copies[k - 1])

    def g_block(j, unused):
        flip_strips(grads2, j, na + j)
        for side in range(2):
            cols = pl.ds(pl.multiple_of(j * block + side * half, half), half)
            wide[...] = jnp.dot(flipped[0], grads2[:, cols], preferred_element_type=full)
            for r in range(chips):
                rows = wide[r * strip : (r + 1) * strip, :]
                g_part[side, slot_of(r, orders[side]), j] = rows.astype(low)
        return unused

    with jax.named_scope("g_block"):
        lax.fori_loop(0, ng, g_block, 0)
        g_copies = start(g_part, g_came, 0)
    with jax.named_scope(f"advance{na - 1}"):
        grad_copies[na - 1] = advance_grad(na - 1, grad_copies[na - 1])
    with jax.named_scope("gather_a"):
        for side in range(2):
            a_copies[side].wait_recv()
        for side in range(2):
            total = a_part[side, 0].astype(full) + a_came[-1][side, 0].astype(full)
            a_rows[mp, :, :, side * half : (side + 1) * half] = total.astype(low)
        gathered = [send(a_rows.at[mp], a_rows.at[mp], (dp, m)) for m in above[1:]]

    with jax.named_scope("cross"):
        for r in range(1, chips):
            for copy in climbed[r - 1]:
                copy.wait_recv()
            where = a_all.at[rows_of(relatives[r], core)]
            crossed.append(send(where, where, partner))
    with jax.named_scope("wait_cross"):
        for copy in crossed:
            copy.wait_recv()

    def finish(k):
        for side in range(2):
            grad_copies[k][side].wait_recv()
            total = grad_part[k, side, 0].astype(full) + grad_came[-1][k, side, 0].astype(full)
            right[side * half : (side + 1) * half, :] = total.astype(low)

        def rows_done(t, unused):
            rows = pl.ds(pl.multiple_of(k * block + t * 256, 256), 256)
            out_tile[rows, :] = jnp.dot(
                a_all[rows, :], right[...], preferred_element_type=full
            ).astype(low)
            return unused

        lax.fori_loop(0, block // 256, rows_done, 0)

    for k in range(na - 1):
        with jax.named_scope(f"finish{k}"):
            finish(k)
    with jax.named_scope("advance_g"):
        g_copies = advance(g_part, g_came, g_copies)
    with jax.named_scope(f"finish{na - 1}"):
        finish(na - 1)

    with jax.named_scope("wait_gather"):
        for copy in gathered:
            copy.wait_recv()
    with jax.named_scope("finish_a"):
        load_old_a.wait()
        for m in range(mp_count):
            rows = slice(m * sub, (m + 1) * sub)
            a_new[:, rows, :] = decay_rate * a_old[:, rows, :] + (1.0 - decay_rate) * a_rows[m].astype(full)
    with jax.named_scope("wait_g"):
        for side in range(2):
            g_copies[side].wait_recv()
    with jax.named_scope("finish_g"):
        load_old_g.wait()
        for side in range(2):
            total = g_part[side, 0].astype(full) + g_came[-1][side, 0].astype(full)
            cols = slice(side * half, (side + 1) * half)
            total = total.astype(low).astype(full)
            g_new[:, :, cols] = decay_rate * g_old[:, :, cols] + (1.0 - decay_rate) * total
    for copy in sent:
        copy.wait_send()


def store(*refs):
    count = len(refs) // 2
    copies = [
        pltpu.make_async_copy(refs[i], refs[count + i], refs[-1].at[i]) for i in range(count)
    ]
    for copy in copies:
        copy.start()
    for copy in copies:
        copy.wait()


def per_device(acts, grads_out, old_a, old_g, a_inverse, g_inverse, owner_map):
    dp_count = lax.axis_size("dp")
    mp_count = lax.axis_size("mp")
    chips = dp_count // 2
    stages = chips.bit_length() - 1
    own, features = acts.shape
    hidden = grads_out.shape[1]
    block = a_inverse.shape[1]
    na, ng = features // block, hidden // block
    strip = block // dp_count
    sub = strip // mp_count
    width = hidden // dp_count
    half = block // 2
    copies = 1 + 2 * na + (chips - 1) * (mp_count + 2) + 1 + (na + 2) * 2 * stages + mp_count - 1
    loads = 5 + block // width // 2

    def came(*shape):
        return [pltpu.VMEM((*shape[0], chips >> (s + 1), *shape[1]), low) for s in range(stages)]

    scratch = [
        pltpu.VMEM((2 * own, features), low),
        pltpu.VMEM((2 * own, hidden), low),
        pltpu.VMEM((hidden, half), low),
        pltpu.VMEM((2 * own, hidden // 2), low),
        pltpu.VMEM((features, block), low),
        pltpu.VMEM((2, half, 2 * own), low),
        pltpu.VMEM((half, half), full),
        pltpu.VMEM((block, width), low),
        pltpu.VMEM((mp_count, na, sub, block), low),
        pltpu.VMEM((na, strip, block), full),
        pltpu.VMEM((ng, strip, block), full),
        pltpu.VMEM((na, 2, chips, half, width), low),
        pltpu.VMEM((2, chips, ng, strip, half), low),
        pltpu.VMEM((2, chips, na, sub, half), low),
        came((na, 2), (half, width)),
        came((2,), (ng, strip, half)),
        came((2,), (na, sub, half)),
        pltpu.SemaphoreType.DMA((loads,)),
        pltpu.SemaphoreType.DMA((copies,)),
        pltpu.SemaphoreType.DMA((copies,)),
    ]
    outside = pl.BlockSpec(memory_space=pltpu.HBM)
    out, a_new, g_new = pl.pallas_call(
        functools.partial(kernel, (dp_count, mp_count, own * dp_count)),
        out_shape=(
            pltpu.VMEM((features, width), low),
            pltpu.VMEM((na, strip, block), full),
            pltpu.VMEM((ng, strip, block), full),
        ),
        in_specs=[pl.BlockSpec(memory_space=pltpu.SMEM)] + [outside] * 6,
        out_specs=(pl.BlockSpec(memory_space=pltpu.VMEM),) * 3,
        scratch_shapes=scratch,
        compiler_params=pltpu.CompilerParams(
            collective_id=0, has_side_effects=True, vmem_limit_bytes=59 * 1024 * 1024 + 7 * 1024 * 100
        ),
        name="step",
    )(owner_map, acts, grads_out, a_inverse, g_inverse, old_a, old_g)
    a_new, g_new, out = pl.pallas_call(
        store,
        out_shape=tuple(jax.ShapeDtypeStruct(x.shape, x.dtype) for x in (a_new, g_new, out)),
        in_specs=[pl.BlockSpec(memory_space=pltpu.VMEM)] * 3,
        out_specs=(pl.BlockSpec(memory_space=pl.ANY),) * 3,
        scratch_shapes=[pltpu.SemaphoreType.DMA((3,))],
        compiler_params=pltpu.CompilerParams(vmem_limit_bytes=1024 * 1024),
        name="store",
    )(a_new, g_new, out)
    return (a_new.reshape(old_a.shape), g_new.reshape(old_g.shape), out.reshape(features, 1, width))


def solution(mesh):
    placed = (
        P("dp", None),
        P("dp", "mp"),
        P("dp", None, None, None),
        P("mp", "dp", None, None, None),
        P("dp", None),
        P("mp", None),
        P(),
    )
    return jax.shard_map(
        per_device,
        mesh=mesh,
        in_specs=placed,
        out_specs=(P("dp", None, None, None), P("mp", "dp", None, None, None), P(None, "mp", "dp")),
        check_vma=False,
    )
```

time: 109 us -> 94.8 us (0.87)
  Pallas kernels: 102 us -> 93.9 us
  other arithmetic: 3.87 us -> 0 us
  local copies, waits for them, and re-layouts: 2.87 us -> 0 us
    pallas_call x1, Pallas kernels: 102 us -> 91.9 us  [per_device(): pl.pallas_call(functools.partial(kernel, (dp_count, mp_count, own * dp_co...]
    unnamed x9 -> x0, local copies, waits for them, and re-layouts: 2.7 us -> none
    add x2 -> x0, other arithmetic: 2.56 us -> none  [the longest x1 1.43 us: per_device(): a_factor = decay_rate * old_a + (1.0 - decay_rate) * a_cov]
    pallas_call x0 -> x1, Pallas kernels: none -> 2.03 us  [per_device(): pl.pallas_call(store, out_shape=tuple((jax.ShapeDtypeStruct(x.shape, x.dt...]
    mul x1 -> x0, other arithmetic: 1.32 us -> none  [per_device(): a_factor = decay_rate * old_a + (1.0 - decay_rate) * a_cov]
where the time goes in v1:
time: 94.8 us; the launch traced here: 94.6 us
  Pallas kernels  93.9 us (99%)
    pallas_call x1, Pallas kernels, per_device(): pl.pallas_call(functools.partial(kernel, (dp_count, mp_count, own * dp_co...  91.9 us
    pallas_call x1, Pallas kernels, per_device(): pl.pallas_call(store, out_shape=tuple((jax.ShapeDtypeStruct(x.shape, x.dt...  2.03 us

profile of v1, /device:TPU:0, one launch (start us, length us, event | category | flops | bytes accessed | tf_op | source)
XLA Modules:
  0.0 94.6 jit_solution(1816327572086983272)
XLA Ops:
  0.6 91.9 %step.1 = (bf16[3072,256]{1,0:T(8,128)(2,1)S(1)}, f32[3,128,1024]{2,1,0:T(8,128)S(1)}, f32[2,128,1024]{2,1,0:T(8,128)S(1)}) custom-call(s32[5,8]{1,0:T(8,128)} %owner_map.1, bf16[512,3072]{1,0:T(8,128)(2,1)} %acts.1, bf16[512,2048]{1,0:T(8,128)(2,1)} %grads.1, bf16[384,1024]{1,0:T(8,128)(2,1)} %a_inverse.1, bf16[2048,1024]{1,0:T(8,128)(2,1)} %g_inverse.1, ...), custom_call_target="tpu_custom_call" | custom-call | tf_op jit(solution)/shard_map/step/pallas_call | solution.py:412
  92.5 2.0 %store.1 = (f32[3,128,1024]{2,1,0:T(8,128)}, f32[2,128,1024]{2,1,0:T(8,128)}, bf16[3072,256]{1,0:T(8,128)(2,1)}) custom-call(f32[3,128,1024]{2,1,0:T(8,128)S(1)} %get-tuple-element.9.refs_0_, f32[2,128,1024]{2,1,0:T(8,128)S(1)} %get-tuple-element.10.refs_1_, bf16[3072,256]{1,0:T(8,128)(2,1)S(1)} %get-tuple-element.11.refs_2_), custom_call_target="tpu_custom_call" | custom-call | tf_op jit(solution)/shard_map/store/pallas_call | solution.py:427

commit v2 on v1

--- a/solution.py
+++ b/solution.py
@@ -29,9 +29,9 @@
 
 
 def kernel(
-    sizes, owner_map, acts, grads, a_inverse, g_inverse, old_a, old_g, out_tile, a_new, g_new,
-    acts2, grads2, g_cols, turned, a_all, flipped, wide, right, a_rows, a_old, g_old,
-    grad_part, g_part, a_part, grad_came, g_came, a_came, local_sem, send_sem, recv_sem,
+    sizes, map_in, acts, grads, a_inverse, g_inverse, old_a, old_g, out_tile, a_new, g_new,
+    acts2, grads2, g_cols, turned, a_all, flipped, wide, right, a_rows, g_rows, a_old, g_old,
+    owner_map, grad_part, g_part, a_part, grad_came, g_came, a_came, sym, local_sem, send_sem, recv_sem,
 ):
     dp_count, mp_count, tokens = sizes
     chips = dp_count // 2
@@ -54,6 +54,7 @@
     chip, core = lax.div(dp, jnp.int32(2)), lax.rem(dp, jnp.int32(2))
     partner = (chip * 2 + 1 - core, mp)
     relatives = [chip_at(chip, r, bits[::-1]) for r in range(chips)]
+    folded = chips == 4 and ng == 2 and strip % 128 == 0
     above = [lax.rem(mp + step, jnp.int32(mp_count)) for step in range(mp_count)]
 
     sent = []
@@ -94,6 +95,7 @@
         for u in range(block // width // 2)
     ]
     load_acts = move(acts, acts2.at[:own])
+    load_map = move(map_in, owner_map)
     load_old_a = move(old_a.at[0], a_old)
     load_old_g = move(old_g.at[0, 0], g_old)
 
@@ -113,7 +115,16 @@
     ]
 
     spread = {}
-    waited = set()
+    climbed = {}
+
+    def arrive(side, held):
+        if (side, held) not in climbed:
+            spread[side, held].wait_recv()
+
+    def climb(side, held):
+        if (side, held) not in climbed:
+            where = (rows_of(relatives[held], core, side), my_piece)
+            climbed[side, held] = [send(a_all.at[where], a_all.at[where], (dp, m)) for m in above[1:]]
 
     def pass_on(stage, relative):
         for side in range(2):
@@ -122,9 +133,10 @@
             peer = (relatives[1 << order[stage]] * 2 + core, mp)
             where = (rows_of(relatives[held], core, side), my_piece)
             if held:
-                spread[side, held].wait_recv()
-                waited.add((side, held))
+                arrive(side, held)
             spread[side, held | (1 << order[stage])] = send(a_all.at[where], a_all.at[where], peer)
+            if held:
+                climb(side, held)
 
     load_inverse.wait()
     for stage in range(stages):
@@ -156,6 +168,13 @@
             add(part, came, stage, copies)
             copies = start(part, came, stage + 1)
         return copies
+
+    def choose(source, block_index, row, owner):
+        rows = None
+        for s in range(dp_count):
+            cols = source[:, pl.ds(pl.multiple_of(block_index * block + s * strip, strip), strip)]
+            rows = cols if rows is None else lax.select(owner_map[row, s] == owner, cols, rows)
+        return rows
 
     def flip_strips(source, block_index, row):
         for r in range(chips):
@@ -255,28 +274,10 @@
         grad_copies[0] = multiply(0)
 
     with jax.named_scope("climb"):
-        climbed = []
         for r in range(1, chips):
             for side in range(2):
-                if (side, r) not in waited:
-                    spread[side, r].wait_recv()
-            where = a_all.at[rows_of(relatives[r], core), my_piece]
-            climbed.append([send(where, where, (dp, m)) for m in above[1:]])
-
-    for k in range(1, na):
-        with jax.named_scope(f"multiply{k}"):
-            grad_copies[k] = multiply(k)
-        if k == 1:
-            with jax.named_scope("a_block"):
-                for later in range(4, 2 * na):
-                    other_acts[later].wait_recv()
-                lax.fori_loop(0, na, a_block, 0)
-                a_copies = start(a_part, a_came, 0)
-        if k == na - 1:
-            with jax.named_scope("advance_a"):
-                a_copies = advance(a_part, a_came, a_copies)
-        with jax.named_scope(f"advance{k - 1}"):
-            grad_copies[k - 1] = advance_grad(k - 1, grad_copies[k - 1])
+                arrive(side, r)
+                climb(side, r)
 
     def g_block(j, unused):
         flip_strips(grads2, j, na + j)
@@ -288,11 +289,128 @@
                 g_part[side, slot_of(r, orders[side]), j] = rows.astype(low)
         return unused
 
-    with jax.named_scope("g_block"):
-        lax.fori_loop(0, ng, g_block, 0)
-        g_copies = start(g_part, g_came, 0)
-    with jax.named_scope(f"advance{na - 1}"):
-        grad_copies[na - 1] = advance_grad(na - 1, grad_copies[na - 1])
+    def start_g():
+        if not folded:
+            lax.fori_loop(0, ng, g_block, 0)
+            return start(g_part, g_came, 0)
+        pick, tile, tile_came, tile_last, fold = sym
+
+        def pick_strip(i, unused):
+            r, other = lax.div(i, jnp.int32(2)), lax.rem(i, jnp.int32(2))
+            owner = chip_at(chip, r, bits[::-1]) * 2 + other
+            rows = choose(grads2, core, na + core, owner)
+            at = pl.ds(pl.multiple_of(i * strip, strip), strip)
+            pick[:, at] = rows
+            flipped[lax.div(i, jnp.int32(dp_count // 2)), pl.ds(
+                pl.multiple_of(lax.rem(i, jnp.int32(dp_count // 2)) * strip, strip), strip
+            ), :] = rows.T
+            return unused
+
+        lax.fori_loop(0, dp_count, pick_strip, 0)
+
+        def product(r, s, first=0, count=2):
+            at = ((r % 2) * 2 + first) * strip
+            lhs = flipped[r // 2, at : at + count * strip, :]
+            rhs = pick[:, s * 2 * strip : (s + 1) * 2 * strip]
+            return jnp.dot(lhs, rhs, preferred_element_type=full).astype(low)
+
+        copies = [None, None]
+        for part in (1, 0):
+            for r in range(chips):
+                for kind, s in enumerate((r, r ^ 3)):
+                    sides = [
+                        side for side in range(2)
+                        if (slot_of(r, orders[side]) >= chips // 2) == bool(part)
+                    ]
+                    if not sides:
+                        continue
+                    value = product(r, s, sides[0], len(sides))
+                    for i, side in enumerate(sides):
+                        place = (0, 1, 3, 4)[slot_of(r, orders[side])]
+                        tile[side, place, kind * strip : (kind + 1) * strip, :] = value[
+                            i * strip : (i + 1) * strip
+                        ]
+            for side in range(2):
+                near, far = 1 << orders[side][0], 1 << orders[side][1]
+                if part:
+                    tile[side, 5] = product(near, 3)
+                    peer = (relatives[near] * 2 + core, mp)
+                    copies[side] = send(tile.at[side, 3:6], tile_came.at[side], peer)
+                else:
+                    tile[side, 2] = product(0, far)
+        return copies
+
+    def advance_g(copies):
+        if not folded:
+            return advance(g_part, g_came, copies)
+        pick, tile, tile_came, tile_last, fold = sym
+        last = []
+        for side in range(2):
+            copies[side].wait_recv()
+
+            def one(i, unused):
+                total = tile[side, i].astype(full) + tile_came[side, i].astype(full)
+                tile[side, i] = total.astype(low)
+                return unused
+
+            lax.fori_loop(0, 3, one, 0)
+            peer = (relatives[1 << orders[side][1]] * 2 + core, mp)
+            last.append(send(tile.at[side, 1:3], tile_last.at[side], peer))
+        return last
+
+    def finish_g(copies):
+        if not folded:
+            for side in range(2):
+                copies[side].wait_recv()
+                total = g_part[side, 0].astype(full) + g_came[-1][side, 0].astype(full)
+                g_rows[:ng, :, side * half : (side + 1) * half] = total.astype(low)
+            return None
+        pick, tile, tile_came, tile_last, fold = sym
+        for side in range(2):
+            copies[side].wait_recv()
+            turned_tile = tile_last[side, 1].astype(full).T
+            fold[side] = tile[side, 2].astype(full) + turned_tile
+            total = tile[side, 0].astype(full) + tile_last[side, 0].astype(full)
+            for kind in range(2):
+                fold[2 + kind, side * strip : (side + 1) * strip, :] = total[
+                    kind * strip : (kind + 1) * strip
+                ]
+        for mine, other in ((1, 1 - core), (0, core)):
+            rows = pl.ds(pl.multiple_of(other * strip, strip), strip)
+            for s in range(dp_count):
+                found = None
+                for r, place in enumerate((2, 1, 0, 3)):
+                    for c in range(2):
+                        value = fold[place, rows, c * strip : (c + 1) * strip]
+                        here = owner_map[na + core, s] == relatives[r] * 2 + c
+                        found = value if found is None else lax.select(here, value, found)
+                g_rows[mine, :, s * strip : (s + 1) * strip] = found.astype(low)
+            if mine:
+                copy = send(g_rows.at[1], g_rows.at[2], partner)
+        return copy
+
+    for k in range(1, na):
+        with jax.named_scope(f"multiply{k}"):
+            grad_copies[k] = multiply(k)
+        if k == 1:
+            with jax.named_scope("a_block"):
+                load_map.wait()
+                for later in range(4, 2 * na):
+                    other_acts[later].wait_recv()
+                lax.fori_loop(0, na, a_block, 0)
+                a_copies = start(a_part, a_came, 0)
+            with jax.named_scope("advance0"):
+                grad_copies[0] = advance_grad(0, grad_copies[0])
+            with jax.named_scope("start_g"):
+                g_copies = start_g()
+            with jax.named_scope("advance_a"):
+                a_copies = advance(a_part, a_came, a_copies)
+        else:
+            with jax.named_scope(f"advance{k - 1}"):
+                grad_copies[k - 1] = advance_grad(k - 1, grad_copies[k - 1])
+
+    with jax.named_scope("advance_g"):
+        g_copies = advance_g(g_copies)
     with jax.named_scope("gather_a"):
         for side in range(2):
             a_copies[side].wait_recv()
@@ -303,10 +421,13 @@
 
     with jax.named_scope("cross"):
         for r in range(1, chips):
-            for copy in climbed[r - 1]:
-                copy.wait_recv()
+            for side in range(2):
+                for copy in climbed[side, r]:
+                    copy.wait_recv()
             where = a_all.at[rows_of(relatives[r], core)]
             crossed.append(send(where, where, partner))
+    with jax.named_scope(f"advance{na - 1}"):
+        grad_copies[na - 1] = advance_grad(na - 1, grad_copies[na - 1])
     with jax.named_scope("wait_cross"):
         for copy in crossed:
             copy.wait_recv()
@@ -329,11 +450,20 @@
     for k in range(na - 1):
         with jax.named_scope(f"finish{k}"):
             finish(k)
-    with jax.named_scope("advance_g"):
-        g_copies = advance(g_part, g_came, g_copies)
-    with jax.named_scope(f"finish{na - 1}"):
-        finish(na - 1)
-
+    with jax.named_scope("finish_g"):
+        swapped = finish_g(g_copies)
+        load_old_g.wait()
+
+        def renew(j, rows):
+            g_new[j] = decay_rate * g_old[j] + (1.0 - decay_rate) * rows.astype(full)
+
+        if folded:
+            renew(core, g_rows[0])
+            swapped.wait_recv()
+            renew(1 - core, g_rows[2])
+        else:
+            for j in range(ng):
+                renew(j, g_rows[j])
     with jax.named_scope("wait_gather"):
         for copy in gathered:
             copy.wait_recv()
@@ -342,16 +472,8 @@
         for m in range(mp_count):
             rows = slice(m * sub, (m + 1) * sub)
             a_new[:, rows, :] = decay_rate * a_old[:, rows, :] + (1.0 - decay_rate) * a_rows[m].astype(full)
-    with jax.named_scope("wait_g"):
-        for side in range(2):
-            g_copies[side].wait_recv()
-    with jax.named_scope("finish_g"):
-        load_old_g.wait()
-        for side in range(2):
-            total = g_part[side, 0].astype(full) + g_came[-1][side, 0].astype(full)
-            cols = slice(side * half, (side + 1) * half)
-            total = total.astype(low).astype(full)
-            g_new[:, :, cols] = decay_rate * g_old[:, :, cols] + (1.0 - decay_rate) * total
+    with jax.named_scope(f"finish{na - 1}"):
+        finish(na - 1)
     for copy in sent:
         copy.wait_send()
 
@@ -380,8 +502,8 @@
     sub = strip // mp_count
     width = hidden // dp_count
     half = block // 2
-    copies = 1 + 2 * na + (chips - 1) * (mp_count + 2) + 1 + (na + 2) * 2 * stages + mp_count - 1
-    loads = 5 + block // width // 2
+    copies = 3 + 2 * na + (chips - 1) * (2 * mp_count + 1) + (na + 2) * 2 * stages + mp_count - 1
+    loads = 6 + block // width // 2
 
     def came(*shape):
         return [pltpu.VMEM((*shape[0], chips >> (s + 1), *shape[1]), low) for s in range(stages)]
@@ -396,14 +518,23 @@
         pltpu.VMEM((half, half), full),
         pltpu.VMEM((block, width), low),
         pltpu.VMEM((mp_count, na, sub, block), low),
+        pltpu.VMEM((max(ng, 3), strip, block), low),
         pltpu.VMEM((na, strip, block), full),
         pltpu.VMEM((ng, strip, block), full),
+        pltpu.SMEM((na + ng, dp_count), jnp.int32),
         pltpu.VMEM((na, 2, chips, half, width), low),
         pltpu.VMEM((2, chips, ng, strip, half), low),
         pltpu.VMEM((2, chips, na, sub, half), low),
         came((na, 2), (half, width)),
         came((2,), (ng, strip, half)),
         came((2,), (na, sub, half)),
+        [
+            pltpu.VMEM((2 * own, block), low),
+            pltpu.VMEM((2, 6, 2 * strip, 2 * strip), low),
+            pltpu.VMEM((2, 3, 2 * strip, 2 * strip), low),
+            pltpu.VMEM((2, 2, 2 * strip, 2 * strip), low),
+            pltpu.VMEM((4, 2 * strip, 2 * strip), full),
+        ],
         pltpu.SemaphoreType.DMA((loads,)),
         pltpu.SemaphoreType.DMA((copies,)),
         pltpu.SemaphoreType.DMA((copies,)),
@@ -416,7 +547,7 @@
             pltpu.VMEM((na, strip, block), full),
             pltpu.VMEM((ng, strip, block), full),
         ),
-        in_specs=[pl.BlockSpec(memory_space=pltpu.SMEM)] + [outside] * 6,
+        in_specs=[outside] * 7,
         out_specs=(pl.BlockSpec(memory_space=pltpu.VMEM),) * 3,
         scratch_shapes=scratch,
         compiler_params=pltpu.CompilerParams(

time: 94.8 us -> 92.5 us (0.976)
  Pallas kernels: 93.9 us -> 91.7 us
    pallas_call x1, Pallas kernels: 91.9 us -> 89.7 us  [per_device(): pl.pallas_call(functools.partial(kernel, (dp_count, mp_count, own * dp_co...]
where the time goes in v2:
time: 92.5 us; the launch traced here: 92.3 us
  Pallas kernels  91.7 us (99%)
    pallas_call x1, Pallas kernels, per_device(): pl.pallas_call(functools.partial(kernel, (dp_count, mp_count, own * dp_co...  89.7 us
    pallas_call x1, Pallas kernels, per_device(): pl.pallas_call(store, out_shape=tuple((jax.ShapeDtypeStruct(x.shape, x.dt...  2.03 us

profile of v2, /device:TPU:0, one launch (start us, length us, event | category | flops | bytes accessed | tf_op | source)
XLA Modules:
  0.0 92.3 jit_solution(5609195940769078787)
XLA Ops:
  0.6 89.7 %step.1 = (bf16[3072,256]{1,0:T(8,128)(2,1)S(1)}, f32[3,128,1024]{2,1,0:T(8,128)S(1)}, f32[2,128,1024]{2,1,0:T(8,128)S(1)}) custom-call(s32[5,8]{1,0:T(8,128)} %map_in.1, bf16[512,3072]{1,0:T(8,128)(2,1)} %acts.1, bf16[512,2048]{1,0:T(8,128)(2,1)} %grads.1, bf16[384,1024]{1,0:T(8,128)(2,1)} %a_inverse.1, bf16[2048,1024]{1,0:T(8,128)(2,1)} %g_inverse.1, ...), custom_call_target="tpu_custom_call" | custom-call | tf_op jit(solution)/shard_map/step/pallas_call | solution.py:543
  90.3 2.0 %store.1 = (f32[3,128,1024]{2,1,0:T(8,128)}, f32[2,128,1024]{2,1,0:T(8,128)}, bf16[3072,256]{1,0:T(8,128)(2,1)}) custom-call(f32[3,128,1024]{2,1,0:T(8,128)S(1)} %get-tuple-element.9.refs_0_, f32[2,128,1024]{2,1,0:T(8,128)S(1)} %get-tuple-element.10.refs_1_, bf16[3072,256]{1,0:T(8,128)(2,1)S(1)} %get-tuple-element.11.refs_2_), custom_call_target="tpu_custom_call" | custom-call | tf_op jit(solution)/shard_map/store/pallas_call | solution.py:558

commit v3 on v2

--- a/solution.py
+++ b/solution.py
@@ -30,7 +30,7 @@
 
 def kernel(
     sizes, map_in, acts, grads, a_inverse, g_inverse, old_a, old_g, out_tile, a_new, g_new,
-    acts2, grads2, g_cols, turned, a_all, flipped, wide, right, a_rows, g_rows, a_old, g_old,
+    acts2, grads2, g_cols, turned, a_all, flipped, wide, right, sofar, a_rows, g_rows, a_old, g_old,
     owner_map, grad_part, g_part, a_part, grad_came, g_came, a_came, sym, local_sem, send_sem, recv_sem,
 ):
     dp_count, mp_count, tokens = sizes
@@ -54,6 +54,10 @@
     chip, core = lax.div(dp, jnp.int32(2)), lax.rem(dp, jnp.int32(2))
     partner = (chip * 2 + 1 - core, mp)
     relatives = [chip_at(chip, r, bits[::-1]) for r in range(chips)]
+    nook = strip + strip // 2
+    one_slot = nook + 2 * strip
+    starts = (0, one_slot, 2 * one_slot + 4 * strip, 3 * one_slot + 4 * strip, 2 * one_slot)
+    starts += (4 * one_slot + 4 * strip,)
     folded = chips == 4 and ng == 2 and strip % 128 == 0
     above = [lax.rem(mp + step, jnp.int32(mp_count)) for step in range(mp_count)]
 
@@ -108,12 +112,6 @@
             pl.semaphore_signal(barrier, inc=1, device_id=peer, device_id_type=pl.DeviceIdType.MESH)
         pl.semaphore_wait(barrier, len(peers))
 
-    other_grads = send(grads, grads2.at[own:], partner)
-    other_acts = [
-        send(acts.at[:, i * half : (i + 1) * half], acts2.at[own:, i * half : (i + 1) * half], partner)
-        for i in range(2 * na)
-    ]
-
     spread = {}
     climbed = {}
 
@@ -141,19 +139,36 @@
     load_inverse.wait()
     for stage in range(stages):
         pass_on(stage, 0)
-    crossed = [send(a_inverse, a_all.at[rows_of(chip, core)], partner)]
-
-    def start_side(part, came, stage, side):
+    other_grads = send(grads, grads2.at[own:], partner)
+    other_acts = []
+
+    def swap_acts(last):
+        for i in range(len(other_acts), last):
+            cols = slice(i * half, (i + 1) * half)
+            other_acts.append(send(acts.at[:, cols], acts2.at[own:, cols], partner))
+
+    swap_acts(2)
+
+    def start_side(part, came, stage, side, slot=None, rows=None):
         first, last = chips >> (stage + 1), chips >> stage
         peer = (relatives[1 << orders[side][stage]] * 2 + core, mp)
-        return send(part.at[side, first:last], came[stage].at[side], peer)
+        src, dst = part.at[side, first:last], came[stage].at[side]
+        if slot is not None:
+            src, dst = part.at[side, slot], came[stage].at[side, slot - first]
+        if rows is not None:
+            src, dst = src.at[:, rows], dst.at[:, rows]
+        return send(src, dst, peer)
 
     def start(part, came, stage):
-        return [start_side(part, came, stage, side) for side in range(2)]
+        return [[start_side(part, came, stage, side)] for side in range(2)]
+
+    def wait_all(copies):
+        for copy in copies:
+            copy.wait_recv()
 
     def add(part, came, stage, copies):
         for side in range(2):
-            copies[side].wait_recv()
+            wait_all(copies[side])
             count = chips >> (stage + 1)
 
             def one(slot, unused):
@@ -163,10 +178,18 @@
 
             lax.fori_loop(0, count, one, 0)
 
-    def advance(part, came, copies):
+    def advance(part, came, copies, split=1):
         for stage in range(stages - 1):
             add(part, came, stage, copies)
-            copies = start(part, came, stage + 1)
+            if stage < stages - 2 or split == 1:
+                copies = start(part, came, stage + 1)
+                continue
+            step = part.shape[2] // split
+            copies = [[], []]
+            for i in range(split):
+                for side in range(2):
+                    rows = slice(i * step, (i + 1) * step)
+                    copies[side].append(start_side(part, came, stage + 1, side, rows=rows))
         return copies
 
     def choose(source, block_index, row, owner):
@@ -215,47 +238,70 @@
         for copy in load_cols:
             copy.wait()
         turn(0)
+    def flip(k, side, first, last):
+        def one(v, unused):
+            cols = pl.ds(pl.multiple_of(k * block + side * half + v * 128, 128), 128)
+            rows = pl.ds(pl.multiple_of(v * 128, 128), 128)
+            flipped[side, rows, first:last] = acts2[first:last, cols].T
+            return unused
+
+        lax.fori_loop(0, half // 128, one, 0)
+
+    with jax.named_scope("flip_own"):
+        load_acts.wait()
+        for side in range(2):
+            flip(0, side, 0, own)
+    with jax.named_scope("turn_other"):
+        other_grads.wait_recv()
+        turn(own)
     with jax.named_scope("pass_on"):
+        swap_acts(2 * na)
         for stage in range(1, stages):
             for relative in range(1, 1 << stage):
                 pass_on(stage, relative)
-    with jax.named_scope("turn_other"):
-        other_grads.wait_recv()
-        turn(own)
+        crossed = [send(a_inverse, a_all.at[rows_of(chip, core)], partner)]
 
     def multiply(k):
         part = grad_part.at[k]
         came = [came.at[k] for came in grad_came]
-        copies = []
-        for first, last in ((chips // 2, chips), (0, chips // 2)):
+
+        def product(side, slot):
+            q = chip_at(chip, slot, orders[side])
+            cols = pl.ds(pl.multiple_of(q * width, width), width)
+            part[side, slot] = jnp.dot(
+                flipped[side], turned[:, cols], preferred_element_type=full
+            ).astype(low)
+
+        def products(side, first, last):
+            def one(slot, unused):
+                product(side, slot)
+                return unused
+
+            lax.fori_loop(first, last, one, 0)
+
+        copies = [[], []]
+        if k == 0:
+            for slot in range(chips - 1, chips // 2 - 1, -1):
+                for side in range(2):
+                    if slot == chips - 1:
+                        other_acts[side].wait_recv()
+                        flip(k, side, own, 2 * own)
+                    product(side, slot)
+                    copies[side].append(start_side(part, came, 0, side, slot))
+        else:
             for side in range(2):
-                if first:
-                    if k < 2:
-                        other_acts[2 * k + side].wait_recv()
-
-                    def flip_one(v, unused):
-                        cols = pl.ds(pl.multiple_of(k * block + side * half + v * 128, 128), 128)
-                        rows = pl.ds(pl.multiple_of(v * 128, 128), 128)
-                        flipped[side, rows, :] = acts2[:, cols].T
-                        return unused
-
-                    lax.fori_loop(0, half // 128, flip_one, 0)
-
-                def product(slot, unused):
-                    q = chip_at(chip, slot, orders[side])
-                    cols = pl.ds(pl.multiple_of(q * width, width), width)
-                    part[side, slot] = jnp.dot(
-                        flipped[side], turned[:, cols], preferred_element_type=full
-                    ).astype(low)
-                    return unused
-
-                lax.fori_loop(first, last, product, 0)
-                if first:
-                    copies.append(start_side(part, came, 0, side))
+                if k == 1:
+                    other_acts[2 * k + side].wait_recv()
+                flip(k, side, 0, 2 * own)
+                products(side, chips // 2, chips)
+                copies[side].append(start_side(part, came, 0, side))
+        for side in range(2):
+            products(side, 0, chips // 2)
         return copies
 
     def advance_grad(k, copies):
-        return advance(grad_part.at[k], [came.at[k] for came in grad_came], copies)
+        split = 2 if k == na - 1 and stages > 1 else 1
+        return advance(grad_part.at[k], [came.at[k] for came in grad_came], copies, split)
 
     def a_block(k, unused):
         flip_strips(acts2, k, k)
@@ -267,8 +313,6 @@
                 a_part[side, slot_of(r, orders[side]), k] = (rows / tokens).astype(low)
         return unused
 
-    with jax.named_scope("wait_acts"):
-        load_acts.wait()
     grad_copies = [None] * na
     with jax.named_scope("multiply0"):
         grad_copies[0] = multiply(0)
@@ -308,36 +352,44 @@
 
         lax.fori_loop(0, dp_count, pick_strip, 0)
 
-        def product(r, s, first=0, count=2):
-            at = ((r % 2) * 2 + first) * strip
-            lhs = flipped[r // 2, at : at + count * strip, :]
-            rhs = pick[:, s * 2 * strip : (s + 1) * 2 * strip]
+        def product(r, first, count, s, col=0, cols=2):
+            at = (r % 2) * 2 * strip + first
+            lhs = flipped[r // 2, at : at + count, :]
+            rhs = pick[:, (s * 2 + col) * strip : (s * 2 + col + cols) * strip]
             return jnp.dot(lhs, rhs, preferred_element_type=full).astype(low)
 
-        copies = [None, None]
-        for part in (1, 0):
-            for r in range(chips):
-                for kind, s in enumerate((r, r ^ 3)):
-                    sides = [
-                        side for side in range(2)
-                        if (slot_of(r, orders[side]) >= chips // 2) == bool(part)
-                    ]
-                    if not sides:
-                        continue
-                    value = product(r, s, sides[0], len(sides))
-                    for i, side in enumerate(sides):
-                        place = (0, 1, 3, 4)[slot_of(r, orders[side])]
-                        tile[side, place, kind * strip : (kind + 1) * strip, :] = value[
-                            i * strip : (i + 1) * strip
-                        ]
+        def slot_tiles(r, side):
+            at = starts[slot_of(r, orders[side])]
+            if side == 0:
+                value = product(r, 0, strip, r)
+                tile[side, at : at + strip] = value[:, :strip]
+                tile[side, at + strip : at + nook] = value[: strip // 2, strip:]
+            else:
+                tile[side, at : at + nook] = product(r, strip // 2, nook, r, 1, 1)
+            value = product(r, side * strip, strip, r ^ 3)
+            for c in range(2):
+                first = at + nook + c * strip
+                tile[side, first : first + strip] = value[:, c * strip : (c + 1) * strip]
+
+        def pair_tile(r, s, side, at):
+            value = product(r, 0, 2 * strip, s)
+            for c in range(2):
+                first = at + c * 2 * strip
+                tile[side, first : first + 2 * strip] = value[:, c * strip : (c + 1) * strip]
+
+        copies = []
+        for upper in (True, False):
             for side in range(2):
                 near, far = 1 << orders[side][0], 1 << orders[side][1]
-                if part:
-                    tile[side, 5] = product(near, 3)
+                for r in range(chips):
+                    if (slot_of(r, orders[side]) >= chips // 2) == upper:
+                        slot_tiles(r, side)
+                if upper:
+                    pair_tile(near, 3, side, starts[5])
                     peer = (relatives[near] * 2 + core, mp)
-                    copies[side] = send(tile.at[side, 3:6], tile_came.at[side], peer)
+                    copies.append(send(tile.at[side, starts[2] :], tile_came.at[side], peer))
                 else:
-                    tile[side, 2] = product(0, far)
+                    pair_tile(0, far, side, starts[4])
         return copies
 
     def advance_g(copies):
@@ -349,32 +401,45 @@
             copies[side].wait_recv()
 
             def one(i, unused):
-                total = tile[side, i].astype(full) + tile_came[side, i].astype(full)
-                tile[side, i] = total.astype(low)
+                rows = pl.ds(pl.multiple_of(i * strip, strip), strip)
+                total = tile[side, rows].astype(full) + tile_came[side, rows].astype(full)
+                tile[side, rows] = total.astype(low)
                 return unused
 
-            lax.fori_loop(0, 3, one, 0)
+            lax.fori_loop(0, starts[2] // strip, one, 0)
             peer = (relatives[1 << orders[side][1]] * 2 + core, mp)
-            last.append(send(tile.at[side, 1:3], tile_last.at[side], peer))
+            last.append(send(tile.at[side, starts[1] : starts[2]], tile_last.at[side], peer))
         return last
 
     def finish_g(copies):
         if not folded:
             for side in range(2):
-                copies[side].wait_recv()
+                wait_all(copies[side])
                 total = g_part[side, 0].astype(full) + g_came[-1][side, 0].astype(full)
                 g_rows[:ng, :, side * half : (side + 1) * half] = total.astype(low)
             return None
         pick, tile, tile_came, tile_last, fold = sym
+        own_tiles = []
         for side in range(2):
             copies[side].wait_recv()
-            turned_tile = tile_last[side, 1].astype(full).T
-            fold[side] = tile[side, 2].astype(full) + turned_tile
-            total = tile[side, 0].astype(full) + tile_last[side, 0].astype(full)
-            for kind in range(2):
-                fold[2 + kind, side * strip : (side + 1) * strip, :] = total[
-                    kind * strip : (kind + 1) * strip
+
+            def whole_tile(ref, at):
+                parts = [ref[side, at + c * 2 * strip : at + (c + 1) * 2 * strip] for c in range(2)]
+                return jnp.concatenate([part.astype(full) for part in parts], axis=1)
+
+            fold[side] = whole_tile(tile, starts[4]) + whole_tile(tile_last, starts[1]).T
+            total = tile[side, : starts[1]].astype(full) + tile_last[side, : starts[1]].astype(full)
+            own_tiles.append(total[:nook])
+            for c in range(2):
+                first = nook + c * strip
+                fold[3, side * strip : (side + 1) * strip, c * strip : (c + 1) * strip] = total[
+                    first : first + strip
                 ]
+        cross = jnp.concatenate([own_tiles[0][strip:], own_tiles[1][: strip // 2]], axis=0)
+        fold[2, :strip, :strip] = own_tiles[0][:strip]
+        fold[2, :strip, strip:] = cross
+        fold[2, strip:, :strip] = cross.T
+        fold[2, strip:, strip:] = own_tiles[1][strip // 2 :]
         for mine, other in ((1, 1 - core), (0, core)):
             rows = pl.ds(pl.multiple_of(other * strip, strip), strip)
             for s in range(dp_count):
@@ -413,7 +478,7 @@
         g_copies = advance_g(g_copies)
     with jax.named_scope("gather_a"):
         for side in range(2):
-            a_copies[side].wait_recv()
+            wait_all(a_copies[side])
         for side in range(2):
             total = a_part[side, 0].astype(full) + a_came[-1][side, 0].astype(full)
             a_rows[mp, :, :, side * half : (side + 1) * half] = total.astype(low)
@@ -433,23 +498,42 @@
             copy.wait_recv()
 
     def finish(k):
-        for side in range(2):
-            grad_copies[k][side].wait_recv()
-            total = grad_part[k, side, 0].astype(full) + grad_came[-1][k, side, 0].astype(full)
-            right[side * half : (side + 1) * half, :] = total.astype(low)
-
-        def rows_done(t, unused):
-            rows = pl.ds(pl.multiple_of(k * block + t * 256, 256), 256)
-            out_tile[rows, :] = jnp.dot(
-                a_all[rows, :], right[...], preferred_element_type=full
-            ).astype(low)
-            return unused
-
-        lax.fori_loop(0, block // 256, rows_done, 0)
+        count = len(grad_copies[k][0]) if k == na - 1 else 1
+        step = half // count
+        for i in range(count):
+            with jax.named_scope(f"finish{k}_{i}"):
+                spans = []
+                for side in range(2):
+                    wait_all(grad_copies[k][side][i : i + 1])
+                    rows = slice(i * step, (i + 1) * step)
+                    total = (
+                        grad_part[k, side, 0, rows].astype(full)
+                        + grad_came[-1][k, side, 0, rows].astype(full)
+                    )
+                    spans.append(slice(side * half + i * step, side * half + (i + 1) * step))
+                    right[spans[-1], :] = total.astype(low)
+                if count == 1:
+                    spans = [slice(0, block)]
+
+                def rows_done(t, unused):
+                    rows = pl.ds(pl.multiple_of(k * block + t * 256, 256), 256)
+                    inner = pl.ds(pl.multiple_of(t * 256, 256), 256)
+                    total = sum(
+                        jnp.dot(a_all[rows, span], right[span, :], preferred_element_type=full)
+                        for span in spans
+                    )
+                    if i:
+                        total = total + sofar[inner, :]
+                    if i < count - 1:
+                        sofar[inner, :] = total
+                    else:
+                        out_tile[rows, :] = total.astype(low)
+                    return unused
+
+                lax.fori_loop(0, block // 256, rows_done, 0)
 
     for k in range(na - 1):
-        with jax.named_scope(f"finish{k}"):
-            finish(k)
+        finish(k)
     with jax.named_scope("finish_g"):
         swapped = finish_g(g_copies)
         load_old_g.wait()
@@ -472,10 +556,10 @@
         for m in range(mp_count):
             rows = slice(m * sub, (m + 1) * sub)
             a_new[:, rows, :] = decay_rate * a_old[:, rows, :] + (1.0 - decay_rate) * a_rows[m].astype(full)
-    with jax.named_scope(f"finish{na - 1}"):
-        finish(na - 1)
-    for copy in sent:
-        copy.wait_send()
+    finish(na - 1)
+    with jax.named_scope("drain"):
+        for copy in sent:
+            copy.wait_send()
 
 
 def store(*refs):
@@ -502,7 +586,7 @@
     sub = strip // mp_count
     width = hidden // dp_count
     half = block // 2
-    copies = 3 + 2 * na + (chips - 1) * (2 * mp_count + 1) + (na + 2) * 2 * stages + mp_count - 1
+    copies = 5 + chips + 2 * na + (chips - 1) * (2 * mp_count + 1) + (na + 2) * 2 * stages + mp_count - 1
     loads = 6 + block // width // 2
 
     def came(*shape):
@@ -517,6 +601,7 @@
         pltpu.VMEM((2, half, 2 * own), low),
         pltpu.VMEM((half, half), full),
         pltpu.VMEM((block, width), low),
+        pltpu.VMEM((block, width), full),
         pltpu.VMEM((mp_count, na, sub, block), low),
         pltpu.VMEM((max(ng, 3), strip, block), low),
         pltpu.VMEM((na, strip, block), full),
@@ -530,9 +615,9 @@
         came((2,), (na, sub, half)),
         [
             pltpu.VMEM((2 * own, block), low),
-            pltpu.VMEM((2, 6, 2 * strip, 2 * strip), low),
-            pltpu.VMEM((2, 3, 2 * strip, 2 * strip), low),
-            pltpu.VMEM((2, 2, 2 * strip, 2 * strip), low),
+            pltpu.VMEM((2, 22 * strip, strip), low),
+            pltpu.VMEM((2, 11 * strip, strip), low),
+            pltpu.VMEM((2, 15 * strip // 2, strip), low),
             pltpu.VMEM((4, 2 * strip, 2 * strip), full),
         ],
         pltpu.SemaphoreType.DMA((loads,)),

time: 92.5 us -> 90.5 us (0.978)
  Pallas kernels: 91.7 us -> 89.5 us
    pallas_call x1, Pallas kernels: 89.7 us -> 87.5 us  [per_device(): pl.pallas_call(functools.partial(kernel, (dp_count, mp_count, own * dp_co...]
where the time goes in v3:
time: 90.5 us; the launch traced here: 90.3 us
  Pallas kernels  89.5 us (99%)
    pallas_call x1, Pallas kernels, per_device(): pl.pallas_call(functools.partial(kernel, (dp_count, mp_count, own * dp_co...  87.5 us
    pallas_call x1, Pallas kernels, per_device(): pl.pallas_call(store, out_shape=tuple((jax.ShapeDtypeStruct(x.shape, x.dt...  2.03 us

profile of v3, /device:TPU:0, one launch (start us, length us, event | category | flops | bytes accessed | tf_op | source)
XLA Modules:
  0.0 90.3 jit_solution(13380793190029708347)
XLA Ops:
  0.6 87.5 %step.1 = (bf16[3072,256]{1,0:T(8,128)(2,1)S(1)}, f32[3,128,1024]{2,1,0:T(8,128)S(1)}, f32[2,128,1024]{2,1,0:T(8,128)S(1)}) custom-call(s32[5,8]{1,0:T(8,128)} %map_in.1, bf16[512,3072]{1,0:T(8,128)(2,1)} %acts.1, bf16[512,2048]{1,0:T(8,128)(2,1)} %grads.1, bf16[384,1024]{1,0:T(8,128)(2,1)} %a_inverse.1, bf16[2048,1024]{1,0:T(8,128)(2,1)} %g_inverse.1, ...), custom_call_target="tpu_custom_call" | custom-call | tf_op jit(solution)/shard_map/step/pallas_call | solution.py:628
  88.1 2.0 %store.1 = (f32[3,128,1024]{2,1,0:T(8,128)}, f32[2,128,1024]{2,1,0:T(8,128)}, bf16[3072,256]{1,0:T(8,128)(2,1)}) custom-call(f32[3,128,1024]{2,1,0:T(8,128)S(1)} %get-tuple-element.9.refs_0_, f32[2,128,1024]{2,1,0:T(8,128)S(1)} %get-tuple-element.10.refs_1_, bf16[3072,256]{1,0:T(8,128)(2,1)S(1)} %get-tuple-element.11.refs_2_), custom_call_target="tpu_custom_call" | custom-call | tf_op jit(solution)/shard_map/store/pallas_call | solution.py:643

commit v4 on v3

--- a/solution.py
+++ b/solution.py
@@ -29,8 +29,8 @@
 
 
 def kernel(
-    sizes, map_in, acts, grads, a_inverse, g_inverse, old_a, old_g, out_tile, a_new, g_new,
-    acts2, grads2, g_cols, turned, a_all, flipped, wide, right, sofar, a_rows, g_rows, a_old, g_old,
+    sizes, map_in, acts, grads, a_inverse, g_inverse, old_a, old_g, out_tile, a_new, g_new, sofar, a_last, right,
+    acts2, grads2, g_cols, turned, a_all, flipped, wide, a_rows, g_rows, a_old, g_old,
     owner_map, grad_part, g_part, a_part, grad_came, g_came, a_came, sym, local_sem, send_sem, recv_sem,
 ):
     dp_count, mp_count, tokens = sizes
@@ -61,17 +61,29 @@
     folded = chips == 4 and ng == 2 and strip % 128 == 0
     above = [lax.rem(mp + step, jnp.int32(mp_count)) for step in range(mp_count)]
 
-    sent = []
-
-    def send(src, dst, device):
-        place = len(sent)
+    out_names, in_names = {}, {}
+
+    def send(src, dst, device, out_name, in_name):
+        out_at = out_names.setdefault(out_name, len(out_names))
+        in_at = in_names.setdefault(in_name, len(in_names))
         copy = pltpu.make_async_remote_copy(
-            src_ref=src, dst_ref=dst, send_sem=send_sem.at[place], recv_sem=recv_sem.at[place],
+            src_ref=src, dst_ref=dst, send_sem=send_sem.at[out_at], recv_sem=recv_sem.at[in_at],
             device_id=device, device_id_type=pl.DeviceIdType.MESH,
         )
         copy.start()
-        sent.append(copy)
-        return copy
+
+    def whole(ref, out_name, in_name):
+        return pltpu.make_async_remote_copy(
+            src_ref=ref, dst_ref=ref, send_sem=send_sem.at[out_names[out_name] if out_name else 0],
+            recv_sem=recv_sem.at[in_names[in_name] if in_name else 0],
+            device_id=partner, device_id_type=pl.DeviceIdType.MESH,
+        )
+
+    def arrived(name, ref):
+        whole(ref, None, name).wait_recv()
+
+    def left(name, ref):
+        whole(ref, name, None).wait_send()
 
     placed = []
 
@@ -112,64 +124,63 @@
             pl.semaphore_signal(barrier, inc=1, device_id=peer, device_id_type=pl.DeviceIdType.MESH)
         pl.semaphore_wait(barrier, len(peers))
 
-    spread = {}
-    climbed = {}
-
-    def arrive(side, held):
-        if (side, held) not in climbed:
-            spread[side, held].wait_recv()
+    climbed = set()
+
+    def piece_of(side, held):
+        return a_all.at[rows_of(relatives[held], core, side), my_piece]
 
     def climb(side, held):
         if (side, held) not in climbed:
-            where = (rows_of(relatives[held], core, side), my_piece)
-            climbed[side, held] = [send(a_all.at[where], a_all.at[where], (dp, m)) for m in above[1:]]
+            climbed.add((side, held))
+            arrived(("spread", side, held), piece_of(side, held))
+            where = piece_of(side, held)
+            for m in above[1:]:
+                send(where, where, (dp, m), "climb", "climb")
 
     def pass_on(stage, relative):
         for side in range(2):
             order = orders[side]
             held = sum(((relative >> i) & 1) << order[i] for i in range(stage))
             peer = (relatives[1 << order[stage]] * 2 + core, mp)
-            where = (rows_of(relatives[held], core, side), my_piece)
-            if held:
-                arrive(side, held)
-            spread[side, held | (1 << order[stage])] = send(a_all.at[where], a_all.at[where], peer)
             if held:
                 climb(side, held)
+            where = piece_of(side, held)
+            name = ("spread", side, held | (1 << order[stage]))
+            send(where, where, peer, "spread", name)
 
     load_inverse.wait()
     for stage in range(stages):
         pass_on(stage, 0)
-    other_grads = send(grads, grads2.at[own:], partner)
-    other_acts = []
-
-    def swap_acts(last):
-        for i in range(len(other_acts), last):
+    send(grads, grads2.at[own:], partner, "grads", "grads")
+
+    def swap_acts(first, last):
+        for i in range(first, last):
             cols = slice(i * half, (i + 1) * half)
-            other_acts.append(send(acts.at[:, cols], acts2.at[own:, cols], partner))
-
-    swap_acts(2)
-
-    def start_side(part, came, stage, side, slot=None, rows=None):
+            name = i if i < 2 else min(i // 2, 2)
+            send(acts.at[:, cols], acts2.at[own:, cols], partner, "acts", ("acts", i < 2, name))
+
+    swap_acts(0, 2)
+
+    def start_side(name, part, came, stage, side, slot=None, rows=None):
         first, last = chips >> (stage + 1), chips >> stage
         peer = (relatives[1 << orders[side][stage]] * 2 + core, mp)
         src, dst = part.at[side, first:last], came[stage].at[side]
         if slot is not None:
             src, dst = part.at[side, slot], came[stage].at[side, slot - first]
+        in_name = (name, stage, 0)
         if rows is not None:
             src, dst = src.at[:, rows], dst.at[:, rows]
-        return send(src, dst, peer)
-
-    def start(part, came, stage):
-        return [[start_side(part, came, stage, side)] for side in range(2)]
-
-    def wait_all(copies):
-        for copy in copies:
-            copy.wait_recv()
-
-    def add(part, came, stage, copies):
-        for side in range(2):
-            wait_all(copies[side])
-            count = chips >> (stage + 1)
+            in_name = (name, stage, rows.start)
+        send(src, dst, peer, name[0], in_name)
+
+    def start(name, part, came, stage):
+        for side in range(2):
+            start_side(name, part, came, stage, side)
+
+    def add(name, part, came, stage):
+        arrived((name, stage, 0), came[stage])
+        count = chips >> (stage + 1)
+        for side in range(2):
 
             def one(slot, unused):
                 total = part[side, slot].astype(full) + came[stage][side, slot].astype(full)
@@ -178,19 +189,17 @@
 
             lax.fori_loop(0, count, one, 0)
 
-    def advance(part, came, copies, split=1):
+    def advance(name, part, came, split=1):
         for stage in range(stages - 1):
-            add(part, came, stage, copies)
+            add(name, part, came, stage)
             if stage < stages - 2 or split == 1:
-                copies = start(part, came, stage + 1)
+                start(name, part, came, stage + 1)
                 continue
             step = part.shape[2] // split
-            copies = [[], []]
             for i in range(split):
                 for side in range(2):
                     rows = slice(i * step, (i + 1) * step)
-                    copies[side].append(start_side(part, came, stage + 1, side, rows=rows))
-        return copies
+                    start_side(name, part, came, stage + 1, side, rows=rows)
 
     def choose(source, block_index, row, owner):
         rows = None
@@ -252,14 +261,14 @@
         for side in range(2):
             flip(0, side, 0, own)
     with jax.named_scope("turn_other"):
-        other_grads.wait_recv()
+        arrived("grads", grads2.at[own:])
         turn(own)
     with jax.named_scope("pass_on"):
-        swap_acts(2 * na)
+        swap_acts(2, 2 * na)
         for stage in range(1, stages):
             for relative in range(1, 1 << stage):
                 pass_on(stage, relative)
-        crossed = [send(a_inverse, a_all.at[rows_of(chip, core)], partner)]
+        send(a_inverse, a_all.at[rows_of(chip, core)], partner, "cross", "cross")
 
     def multiply(k):
         part = grad_part.at[k]
@@ -279,29 +288,25 @@
 
             lax.fori_loop(first, last, one, 0)
 
-        copies = [[], []]
         if k == 0:
             for slot in range(chips - 1, chips // 2 - 1, -1):
                 for side in range(2):
                     if slot == chips - 1:
-                        other_acts[side].wait_recv()
+                        arrived(("acts", True, side), acts2.at[own:, side * half : (side + 1) * half])
                         flip(k, side, own, 2 * own)
                     product(side, slot)
-                    copies[side].append(start_side(part, came, 0, side, slot))
+                    start_side(("grad", k), part, came, 0, side, slot)
         else:
             for side in range(2):
-                if k == 1:
-                    other_acts[2 * k + side].wait_recv()
                 flip(k, side, 0, 2 * own)
                 products(side, chips // 2, chips)
-                copies[side].append(start_side(part, came, 0, side))
+                start_side(("grad", k), part, came, 0, side)
         for side in range(2):
             products(side, 0, chips // 2)
-        return copies
-
-    def advance_grad(k, copies):
+
+    def advance_grad(k):
         split = 2 if k == na - 1 and stages > 1 else 1
-        return advance(grad_part.at[k], [came.at[k] for came in grad_came], copies, split)
+        advance(("grad", k), grad_part.at[k], [came.at[k] for came in grad_came], split)
 
     def a_block(k, unused):
         flip_strips(acts2, k, k)
@@ -313,14 +318,12 @@
                 a_part[side, slot_of(r, orders[side]), k] = (rows / tokens).astype(low)
         return unused
 
-    grad_copies = [None] * na
     with jax.named_scope("multiply0"):
-        grad_copies[0] = multiply(0)
+        multiply(0)
 
     with jax.named_scope("climb"):
         for r in range(1, chips):
             for side in range(2):
-                arrive(side, r)
                 climb(side, r)
 
     def g_block(j, unused):
@@ -336,7 +339,8 @@
     def start_g():
         if not folded:
             lax.fori_loop(0, ng, g_block, 0)
-            return start(g_part, g_came, 0)
+            start(("g",), g_part, g_came, 0)
+            return
         pick, tile, tile_came, tile_last, fold = sym
 
         def pick_strip(i, unused):
@@ -377,7 +381,6 @@
                 first = at + c * 2 * strip
                 tile[side, first : first + 2 * strip] = value[:, c * strip : (c + 1) * strip]
 
-        copies = []
         for upper in (True, False):
             for side in range(2):
                 near, far = 1 << orders[side][0], 1 << orders[side][1]
@@ -387,18 +390,17 @@
                 if upper:
                     pair_tile(near, 3, side, starts[5])
                     peer = (relatives[near] * 2 + core, mp)
-                    copies.append(send(tile.at[side, starts[2] :], tile_came.at[side], peer))
+                    send(tile.at[side, starts[2] :], tile_came.at[side], peer, "g", "tile0")
                 else:
                     pair_tile(0, far, side, starts[4])
-        return copies
-
-    def advance_g(copies):
+
+    def advance_g():
         if not folded:
-            return advance(g_part, g_came, copies)
+            advance(("g",), g_part, g_came)
+            return
         pick, tile, tile_came, tile_last, fold = sym
-        last = []
-        for side in range(2):
-            copies[side].wait_recv()
+        arrived("tile0", tile_came)
+        for side in range(2):
 
             def one(i, unused):
                 rows = pl.ds(pl.multiple_of(i * strip, strip), strip)
@@ -408,20 +410,19 @@
 
             lax.fori_loop(0, starts[2] // strip, one, 0)
             peer = (relatives[1 << orders[side][1]] * 2 + core, mp)
-            last.append(send(tile.at[side, starts[1] : starts[2]], tile_last.at[side], peer))
-        return last
-
-    def finish_g(copies):
+            send(tile.at[side, starts[1] : starts[2]], tile_last.at[side], peer, "g", "tile1")
+
+    def finish_g():
         if not folded:
+            arrived((("g",), stages - 1, 0), g_came[-1])
             for side in range(2):
-                wait_all(copies[side])
                 total = g_part[side, 0].astype(full) + g_came[-1][side, 0].astype(full)
                 g_rows[:ng, :, side * half : (side + 1) * half] = total.astype(low)
-            return None
+            return
         pick, tile, tile_came, tile_last, fold = sym
         own_tiles = []
-        for side in range(2):
-            copies[side].wait_recv()
+        arrived("tile1", tile_last)
+        for side in range(2):
 
             def whole_tile(ref, at):
                 parts = [ref[side, at + c * 2 * strip : at + (c + 1) * 2 * strip] for c in range(2)]
@@ -451,91 +452,88 @@
                         found = value if found is None else lax.select(here, value, found)
                 g_rows[mine, :, s * strip : (s + 1) * strip] = found.astype(low)
             if mine:
-                copy = send(g_rows.at[1], g_rows.at[2], partner)
-        return copy
+                send(g_rows.at[1], g_rows.at[2], partner, "rows", "rows")
 
     for k in range(1, na):
         with jax.named_scope(f"multiply{k}"):
-            grad_copies[k] = multiply(k)
+            if k == 1:
+                arrived(("acts", False, 1), acts2.at[own:, block : 2 * block])
+            multiply(k)
         if k == 1:
             with jax.named_scope("a_block"):
                 load_map.wait()
-                for later in range(4, 2 * na):
-                    other_acts[later].wait_recv()
+                if na > 2:
+                    arrived(("acts", False, 2), acts2.at[own:, 2 * block :])
                 lax.fori_loop(0, na, a_block, 0)
-                a_copies = start(a_part, a_came, 0)
+                start(("a",), a_part, a_came, 0)
             with jax.named_scope("advance0"):
-                grad_copies[0] = advance_grad(0, grad_copies[0])
+                advance_grad(0)
             with jax.named_scope("start_g"):
-                g_copies = start_g()
+                start_g()
             with jax.named_scope("advance_a"):
-                a_copies = advance(a_part, a_came, a_copies)
+                advance(("a",), a_part, a_came)
         else:
             with jax.named_scope(f"advance{k - 1}"):
-                grad_copies[k - 1] = advance_grad(k - 1, grad_copies[k - 1])
+                advance_grad(k - 1)
 
     with jax.named_scope("advance_g"):
-        g_copies = advance_g(g_copies)
+        advance_g()
     with jax.named_scope("gather_a"):
-        for side in range(2):
-            wait_all(a_copies[side])
+        arrived((("a",), stages - 1, 0), a_came[-1])
         for side in range(2):
             total = a_part[side, 0].astype(full) + a_came[-1][side, 0].astype(full)
             a_rows[mp, :, :, side * half : (side + 1) * half] = total.astype(low)
-        gathered = [send(a_rows.at[mp], a_rows.at[mp], (dp, m)) for m in above[1:]]
-
+        for m in above[1:]:
+            send(a_rows.at[mp], a_rows.at[mp], (dp, m), "gather", "gather")
+
+    climbing = a_all.at[: (chips - 1) * shard, : (mp_count - 1) * piece]
     with jax.named_scope("cross"):
+        arrived("climb", climbing)
         for r in range(1, chips):
-            for side in range(2):
-                for copy in climbed[side, r]:
-                    copy.wait_recv()
             where = a_all.at[rows_of(relatives[r], core)]
-            crossed.append(send(where, where, partner))
+            send(where, where, partner, "cross", "cross")
     with jax.named_scope(f"advance{na - 1}"):
-        grad_copies[na - 1] = advance_grad(na - 1, grad_copies[na - 1])
+        advance_grad(na - 1)
     with jax.named_scope("wait_cross"):
-        for copy in crossed:
-            copy.wait_recv()
-
-    def finish(k):
-        count = len(grad_copies[k][0]) if k == na - 1 else 1
+        arrived("cross", a_all.at[: chips * shard])
+
+    def finish(k, piece_index=0, count=1):
         step = half // count
-        for i in range(count):
-            with jax.named_scope(f"finish{k}_{i}"):
-                spans = []
-                for side in range(2):
-                    wait_all(grad_copies[k][side][i : i + 1])
-                    rows = slice(i * step, (i + 1) * step)
-                    total = (
-                        grad_part[k, side, 0, rows].astype(full)
-                        + grad_came[-1][k, side, 0, rows].astype(full)
-                    )
-                    spans.append(slice(side * half + i * step, side * half + (i + 1) * step))
-                    right[spans[-1], :] = total.astype(low)
-                if count == 1:
-                    spans = [slice(0, block)]
-
-                def rows_done(t, unused):
-                    rows = pl.ds(pl.multiple_of(k * block + t * 256, 256), 256)
-                    inner = pl.ds(pl.multiple_of(t * 256, 256), 256)
-                    total = sum(
-                        jnp.dot(a_all[rows, span], right[span, :], preferred_element_type=full)
-                        for span in spans
-                    )
-                    if i:
-                        total = total + sofar[inner, :]
-                    if i < count - 1:
-                        sofar[inner, :] = total
-                    else:
-                        out_tile[rows, :] = total.astype(low)
-                    return unused
-
-                lax.fori_loop(0, block // 256, rows_done, 0)
+        spans = []
+        name = (("grad", k), stages - 1, piece_index * step)
+        rows = slice(piece_index * step, (piece_index + 1) * step)
+        arrived(name, grad_came[-1].at[k, :, :, rows])
+        for side in range(2):
+            total = (
+                grad_part[k, side, 0, rows].astype(full) + grad_came[-1][k, side, 0, rows].astype(full)
+            )
+            spans.append(slice(side * half + rows.start, side * half + rows.stop))
+            right[spans[-1], :] = total.astype(low)
+        if piece_index:
+            return
+        if count == 1:
+            spans = [slice(0, block)]
+
+        def rows_done(t, unused):
+            rows = pl.ds(pl.multiple_of(k * block + t * 256, 256), 256)
+            inner = pl.ds(pl.multiple_of(t * 256, 256), 256)
+            total = sum(
+                jnp.dot(a_all[rows, span], right[span, :], preferred_element_type=full)
+                for span in spans
+            )
+            if count > 1:
+                sofar[inner, :] = total
+                a_last[inner, :] = a_all[rows, :]
+            else:
+                out_tile[rows, :] = total.astype(low)
+            return unused
+
+        lax.fori_loop(0, block // 256, rows_done, 0)
 
     for k in range(na - 1):
         finish(k)
     with jax.named_scope("finish_g"):
-        swapped = finish_g(g_copies)
+        finish_g()
         load_old_g.wait()
 
         def renew(j, rows):
@@ -543,32 +541,61 @@
 
         if folded:
             renew(core, g_rows[0])
-            swapped.wait_recv()
+            arrived("rows", g_rows.at[2])
             renew(1 - core, g_rows[2])
         else:
             for j in range(ng):
                 renew(j, g_rows[j])
     with jax.named_scope("wait_gather"):
-        for copy in gathered:
-            copy.wait_recv()
+        arrived("gather", a_rows.at[: mp_count - 1])
     with jax.named_scope("finish_a"):
         load_old_a.wait()
         for m in range(mp_count):
             rows = slice(m * sub, (m + 1) * sub)
             a_new[:, rows, :] = decay_rate * a_old[:, rows, :] + (1.0 - decay_rate) * a_rows[m].astype(full)
-    finish(na - 1)
+    with jax.named_scope("finish_first"):
+        finish(na - 1, 0, 2)
+    with jax.named_scope("finish_last"):
+        finish(na - 1, 1, 2)
     with jax.named_scope("drain"):
-        for copy in sent:
-            copy.wait_send()
-
-
-def store(*refs):
-    count = len(refs) // 2
+        left("grads", grads2.at[own:])
+        left("acts", acts2.at[own:])
+        left("spread", a_all.at[: (chips - 1) * shard, :piece])
+        left("climb", climbing)
+        left("cross", a_all.at[: chips * shard])
+        left("grad", grad_part.at[:, :, : chips - 1])
+        left("a", a_part.at[:, : chips - 1])
+        if folded:
+            left("g", sym[1].at[:, : 2 * starts[2] - starts[1]])
+            left("rows", g_rows.at[1])
+        else:
+            left("g", g_part.at[:, : chips - 1])
+        left("gather", a_rows.at[: mp_count - 1])
+
+
+def store(first, a_new, g_new, sofar, a_last, right, out, a_out, g_out, last, sem):
     copies = [
-        pltpu.make_async_copy(refs[i], refs[count + i], refs[-1].at[i]) for i in range(count)
+        pltpu.make_async_copy(a_new, a_out, sem.at[0]),
+        pltpu.make_async_copy(g_new, g_out, sem.at[1]),
+        pltpu.make_async_copy(first, out.at[: first.shape[0]], sem.at[2]),
     ]
     for copy in copies:
         copy.start()
+    block = a_last.shape[0]
+    quarter = block // 4
+
+    def one(t, unused):
+        rows = pl.ds(pl.multiple_of(t * 256, 256), 256)
+        total = sofar[rows, :]
+        for begin in (quarter, 3 * quarter):
+            span = slice(begin, begin + quarter)
+            total += jnp.dot(a_last[rows, span], right[span, :], preferred_element_type=full)
+        last[rows, :] = total.astype(low)
+        return unused
+
+    lax.fori_loop(0, block // 256, one, 0)
+    copies.append(pltpu.make_async_copy(last, out.at[first.shape[0] :], sem.at[3]))
+    copies[-1].start()
     for copy in copies:
         copy.wait()
 
@@ -586,7 +613,8 @@
     sub = strip // mp_count
     width = hidden // dp_count
     half = block // 2
-    copies = 5 + chips + 2 * na + (chips - 1) * (2 * mp_count + 1) + (na + 2) * 2 * stages + mp_count - 1
+    names_out = 10
+    names_in = 9 + 2 * (chips - 1) + (na + 2) * stages + 1
     loads = 6 + block // width // 2
 
     def came(*shape):
@@ -600,8 +628,6 @@
         pltpu.VMEM((features, block), low),
         pltpu.VMEM((2, half, 2 * own), low),
         pltpu.VMEM((half, half), full),
-        pltpu.VMEM((block, width), low),
-        pltpu.VMEM((block, width), full),
         pltpu.VMEM((mp_count, na, sub, block), low),
         pltpu.VMEM((max(ng, 3), strip, block), low),
         pltpu.VMEM((na, strip, block), full),
@@ -621,34 +647,41 @@
             pltpu.VMEM((4, 2 * strip, 2 * strip), full),
         ],
         pltpu.SemaphoreType.DMA((loads,)),
-        pltpu.SemaphoreType.DMA((copies,)),
-        pltpu.SemaphoreType.DMA((copies,)),
+        pltpu.SemaphoreType.DMA((names_out,)),
+        pltpu.SemaphoreType.DMA((names_in,)),
     ]
     outside = pl.BlockSpec(memory_space=pltpu.HBM)
-    out, a_new, g_new = pl.pallas_call(
+    results = pl.pallas_call(
         functools.partial(kernel, (dp_count, mp_count, own * dp_count)),
         out_shape=(
-            pltpu.VMEM((features, width), low),
+            pltpu.VMEM((features - block, width), low),
             pltpu.VMEM((na, strip, block), full),
             pltpu.VMEM((ng, strip, block), full),
+            pltpu.VMEM((block, width), full),
+            pltpu.VMEM((block, block), low),
+            pltpu.VMEM((block, width), low),
         ),
         in_specs=[outside] * 7,
-        out_specs=(pl.BlockSpec(memory_space=pltpu.VMEM),) * 3,
+        out_specs=(pl.BlockSpec(memory_space=pltpu.VMEM),) * 6,
         scratch_shapes=scratch,
         compiler_params=pltpu.CompilerParams(
-            collective_id=0, has_side_effects=True, vmem_limit_bytes=59 * 1024 * 1024 + 7 * 1024 * 100
+            collective_id=0, has_side_effects=True, vmem_limit_bytes=57 * 1024 * 1024 - 300 * 1024
         ),
         name="step",
     )(owner_map, acts, grads_out, a_inverse, g_inverse, old_a, old_g)
-    a_new, g_new, out = pl.pallas_call(
+    out, a_new, g_new = pl.pallas_call(
         store,
-        out_shape=tuple(jax.ShapeDtypeStruct(x.shape, x.dtype) for x in (a_new, g_new, out)),
-        in_specs=[pl.BlockSpec(memory_space=pltpu.VMEM)] * 3,
+        out_shape=(
+            jax.ShapeDtypeStruct((features, width), low),
+            jax.ShapeDtypeStruct((na, strip, block), full),
+            jax.ShapeDtypeStruct((ng, strip, block), full),
+        ),
+        in_specs=[pl.BlockSpec(memory_space=pltpu.VMEM)] * 6,
         out_specs=(pl.BlockSpec(memory_space=pl.ANY),) * 3,
-        scratch_shapes=[pltpu.SemaphoreType.DMA((3,))],
-        compiler_params=pltpu.CompilerParams(vmem_limit_bytes=1024 * 1024),
+        scratch_shapes=[pltpu.VMEM((block, width), low), pltpu.SemaphoreType.DMA((4,))],
+        compiler_params=pltpu.CompilerParams(vmem_limit_bytes=8 * 1024 * 1024),
         name="store",
-    )(a_new, g_new, out)
+    )(*results)
     return (a_new.reshape(old_a.shape), g_new.reshape(old_g.shape), out.reshape(features, 1, width))
 
 

time: 90.5 us -> 88.7 us (0.980)
  Pallas kernels: 89.5 us -> 87.7 us
    pallas_call x1, Pallas kernels: 87.5 us -> 85.7 us  [per_device(): pl.pallas_call(functools.partial(kernel, (dp_count, mp_count, own * dp_co...]
where the time goes in v4:
time: 88.7 us; the launch traced here: 88.5 us
  Pallas kernels  87.7 us (99%)
    pallas_call x1, Pallas kernels, per_device(): pl.pallas_call(functools.partial(kernel, (dp_count, mp_count, own * dp_co...  85.7 us
    pallas_call x1, Pallas kernels, per_device(): pl.pallas_call(store, out_shape=(jax.ShapeDtypeStruct((features, width),...  2.04 us

profile of v4, /device:TPU:0, one launch (start us, length us, event | category | flops | bytes accessed | tf_op | source)
XLA Modules:
  0.0 88.5 jit_solution(13884185413224654359)
XLA Ops:
  0.6 85.7 %step.1 = (bf16[2048,256]{1,0:T(8,128)(2,1)S(1)}, f32[3,128,1024]{2,1,0:T(8,128)S(1)}, f32[2,128,1024]{2,1,0:T(8,128)S(1)}, f32[1024,256]{1,0:T(8,128)S(1)}, bf1...) custom-call(s32[5,8]{1,0:T(8,128)} %map_in.1, bf16[512,3072]{1,0:T(8,128)(2,1)} %acts.1, ...), custom_call_target="tpu_custom_call" | custom-call | tf_op jit(solution)/shard_map/step/pallas_call | solution.py:654
  86.3 2.0 %store.1 = (bf16[3072,256]{1,0:T(8,128)(2,1)}, f32[3,128,1024]{2,1,0:T(8,128)}, f32[2,128,1024]{2,1,0:T(8,128)}) custom-call(bf16[2048,256]{1,0:T(8,128)(2,1)S(1)} %get-tuple-element.12.first, f32[3,128,1024]{2,1,0:T(8,128)S(1)} %get-tuple-element.13.a_new, f32[2,128,1024]{2,1,0:T(8,128)S(1)} %get-tuple-element.14.g_new, ...), custom_call_target="tpu_custom_call" | custom-call | tf_op jit(solution)/shard_map/store/pallas_call | solution.py:672

commit v5 on v4

--- a/solution.py
+++ b/solution.py
@@ -231,22 +231,22 @@
                 chosen = lax.select(here == 1, part, chosen)
             flipped[0, r * strip : (r + 1) * strip, :] = chosen
 
-    def turn(first):
-        def one(j, unused):
-            rows = pl.ds(pl.multiple_of(j * block, block), block)
-            cols = pl.ds(pl.multiple_of(j * half, half), half)
-            turned[first : first + own, cols] = jnp.dot(
-                grads2[first : first + own, rows], g_cols[rows, :], preferred_element_type=full
+    def turn(first, *chosen):
+        per_block = half // width
+        for r in chosen:
+            q = relatives[r]
+            rows = pl.ds(pl.multiple_of(lax.div(q, jnp.int32(per_block)) * block, block), block)
+            inner = pl.ds(pl.multiple_of(lax.rem(q, jnp.int32(per_block)) * width, width), width)
+            turned[first : first + own, pl.ds(pl.multiple_of(q * width, width), width)] = jnp.dot(
+                grads2[first : first + own, rows], g_cols[rows, inner], preferred_element_type=full
             ).astype(low)
-            return unused
-
-        lax.fori_loop(0, ng, one, 0)
 
     with jax.named_scope("turn_own"):
         load_grads.wait()
         for copy in load_cols:
             copy.wait()
-        turn(0)
+        turn(0, chips - 1)
+
     def flip(k, side, first, last):
         def one(v, unused):
             cols = pl.ds(pl.multiple_of(k * block + side * half + v * 128, 128), 128)
@@ -262,7 +262,7 @@
             flip(0, side, 0, own)
     with jax.named_scope("turn_other"):
         arrived("grads", grads2.at[own:])
-        turn(own)
+        turn(own, chips - 1)
     with jax.named_scope("pass_on"):
         swap_acts(2, 2 * na)
         for stage in range(1, stages):
@@ -290,6 +290,9 @@
 
         if k == 0:
             for slot in range(chips - 1, chips // 2 - 1, -1):
+                if slot == chips - 2:
+                    for tokens_at in (0, own):
+                        turn(tokens_at, *range(chips - 1))
                 for side in range(2):
                     if slot == chips - 1:
                         arrived(("acts", True, side), acts2.at[own:, side * half : (side + 1) * half])

time: 88.7 us -> 88.1 us (level)
  no operation moved by 1% of the time
where the time goes in v5:
time: 88.1 us; the launch traced here: 87.9 us
  Pallas kernels  87.1 us (99%)
    pallas_call x1, Pallas kernels, per_device(): pl.pallas_call(functools.partial(kernel, (dp_count, mp_count, own * dp_co...  85.1 us
    pallas_call x1, Pallas kernels, per_device(): pl.pallas_call(store, out_shape=(jax.ShapeDtypeStruct((features, width),...  2.04 us

profile of v5, /device:TPU:0, one launch (start us, length us, event | category | flops | bytes accessed | tf_op | source)
XLA Modules:
  0.0 87.9 jit_solution(16570271491319668648)
XLA Ops:
  0.6 85.1 %step.1 = (bf16[2048,256]{1,0:T(8,128)(2,1)S(1)}, f32[3,128,1024]{2,1,0:T(8,128)S(1)}, f32[2,128,1024]{2,1,0:T(8,128)S(1)}, f32[1024,256]{1,0:T(8,128)S(1)}, bf1...) custom-call(s32[5,8]{1,0:T(8,128)} %map_in.1, bf16[512,3072]{1,0:T(8,128)(2,1)} %acts.1, ...), custom_call_target="tpu_custom_call" | custom-call | tf_op jit(solution)/shard_map/step/pallas_call | solution.py:657
  85.7 2.0 %store.1 = (bf16[3072,256]{1,0:T(8,128)(2,1)}, f32[3,128,1024]{2,1,0:T(8,128)}, f32[2,128,1024]{2,1,0:T(8,128)}) custom-call(bf16[2048,256]{1,0:T(8,128)(2,1)S(1)} %get-tuple-element.12.first, f32[3,128,1024]{2,1,0:T(8,128)S(1)} %get-tuple-element.13.a_new, f32[2,128,1024]{2,1,0:T(8,128)S(1)} %get-tuple-element.14.g_new, ...), custom_call_target="tpu_custom_call" | custom-call | tf_op jit(solution)/shard_map/store/pallas_call | solution.py:675
